TPU v7x, 256 devices: a whole 4x4x8 slice. The times are simulated.
256 devices in a mesh: dp: 16 (over z_lo, x, core), tensor: 16 (over z_hi, y).
Axes of the slice: x: 4, y: 4, z: 8 (z_hi: 4, z_lo: 2; z = z_hi * 2 + z_lo), core: 2. Of those that a mesh axis runs over, the one named last changes fastest.
Arguments:
- activations: bfloat16 [4096, 5120], P('dp'), may hold values from -6 to 6
- grad_out: bfloat16 [4096, 5120], P('dp'), may hold values from -6 to 6
- gate_pre: bfloat16 [4096, 7168], P('dp', 'tensor'), may hold values from -8 to 8
- up_pre: bfloat16 [4096, 7168], P('dp', 'tensor'), may hold values from -6 to 6
- gate_up: bfloat16 [5120, 2, 7168], P('dp', None, 'tensor'), may hold values from -0.078125 to 0.078125
- down_weight: bfloat16 [5120, 7168], P('dp', 'tensor'), may hold values from -0.0625 to 0.0625
Outputs:
- grad_input: bfloat16 [4096, 5120], P('dp')
- grad_gate_up: float32 [5120, 2, 7168], P('dp', None, 'tensor')
- grad_down: float32 [5120, 7168], P('dp', 'tensor')
All inputs are finite; a program needn't handle non-finite values.
Results may differ from a plain program's by a relative error of at most 0.017.
Values may be sent and summed in bfloat16 or wider, within the bound.
No kernel may reach another device: no remote copies, remote signals or barrier semaphores. Data moves between devices by JAX's collectives and lax.ppermute only.
A program may use at most 128 MiB of HBM per device.

v0:
```python
import functools

import jax
import jax.numpy as jnp
from jax import lax
from jax.experimental import pallas as pl
from jax.experimental.pallas import tpu as pltpu
from jax.sharding import Mesh
from jax.sharding import PartitionSpec as P

Z, X, C = "dp_0", "dp_1", "dp_2"
DP = (Z, X, C)
ZH, Y = "tensor_0", "tensor_1"
TENSOR = (ZH, Y)
BF = jnp.bfloat16
F32 = jnp.float32


def shift(v, axis, step):
    n = lax.axis_size(axis)
    return lax.ppermute(v, axis, [(i, (i + step) % n) for i in range(n)])


def ring(v):
    n = lax.axis_size(X)
    pairs = []
    for i in range(n):
        pairs.append((2 * i, 2 * ((i + 1) % n)))
        pairs.append((2 * i + 1, 2 * ((i - 1) % n) + 1))
    return lax.ppermute(v, (X, C), pairs)


def swap(v, axis):
    return lax.ppermute(v, axis, [(0, 1), (1, 0)])


def to_columns_kernel(pos_ref, x_ref, mine_ref, theirs_ref, *, slab):
    for core in range(2):

        @pl.when(pos_ref[1] == core)
        def _(core=core):
            for k in range(x_ref.shape[1] // (2 * slab)):
                for ref, side in ((mine_ref, core), (theirs_ref, 1 - core)):
                    at = (2 * k + side) * slab
                    ref[:, k * slab : (k + 1) * slab] = x_ref[:, at : at + slab]


def to_columns(x, pos, slab):
    tokens, width = x.shape
    rows = 64
    out = jax.ShapeDtypeStruct((tokens, width // 2), x.dtype)
    return pl.pallas_call(
        functools.partial(to_columns_kernel, slab=slab),
        grid_spec=pltpu.PrefetchScalarGridSpec(
            num_scalar_prefetch=1,
            grid=(tokens // rows,),
            in_specs=[pl.BlockSpec((rows, width), lambda i, s: (i, 0))],
            out_specs=[pl.BlockSpec((rows, width // 2), lambda i, s: (i, 0))] * 2,
        ),
        out_shape=[out, out],
        name="to_columns",
    )(pos, x)


def factors_kernel(own_ref, other_ref, hidden_ref, gate_ref, up_ref):
    width = hidden_ref.shape[0]
    tokens = own_ref.shape[1]
    for a, ref in enumerate((own_ref, other_ref)):
        at = slice(a * tokens, (a + 1) * tokens)
        g = ref[:width].astype(F32)
        u = ref[width:].astype(F32)
        s = 1.0 / (1.0 + jnp.exp(-g))
        silu = g * s
        hidden_ref[:, at] = (silu * u).astype(BF)
        gate_ref[:, at] = u * s * (1.0 + g * (1.0 - s))
        up_ref[:, at] = silu


def factors(own, other):
    width, tokens = own.shape
    outs = [jax.ShapeDtypeStruct((width // 2, 2 * tokens), t) for t in (BF, F32, F32)]
    return pl.pallas_call(factors_kernel, out_shape=outs, name="factors")(own, other)


def grad_hidden_kernel(part_ref, got_ref, gate_ref, up_ref, o_ref):
    width, both = part_ref.shape
    tokens = both // 2
    for a in range(2):
        at = slice(a * tokens, (a + 1) * tokens)
        h = part_ref[:, at] + got_ref[:, tokens - a * tokens : both - a * tokens]
        o_ref[:width, at] = (h * gate_ref[:, at]).astype(BF)
        o_ref[width:, at] = (h * up_ref[:, at]).astype(BF)


def grad_hidden_of(part, got, gate, up):
    width, both = part.shape
    return pl.pallas_call(
        grad_hidden_kernel,
        out_shape=jax.ShapeDtypeStruct((2 * width, both), BF),
        name="grad_hidden",
    )(part, got, gate, up)


def cut_kernel(pos_ref, x_ref, *o_refs):
    n = len(o_refs)
    for j, o_ref in enumerate(o_refs):
        at = (pos_ref[3] + j) & (n - 1)
        for a in range(2):
            o_ref[:, a] = x_ref[a, at]


def cut(x, pos, n, m, rows):
    cols = x.shape[1]
    out = jax.ShapeDtypeStruct((m, 2, rows, cols), x.dtype)
    outs = pl.pallas_call(
        cut_kernel,
        in_specs=[
            pl.BlockSpec(memory_space=pltpu.SMEM),
            pl.BlockSpec(memory_space=pltpu.VMEM),
        ],
        out_shape=[out] * n,
        name="cut",
    )(pos, x.reshape(2, n, m, rows, cols))
    return [o.reshape(m * 2 * rows, cols) for o in outs]


def from_slabs_kernel(pos_ref, own_ref, other_ref, o_ref, *, slab):
    core_odd = pos_ref[1] == 1
    own, other = own_ref[...], other_ref[...]
    for i in range(own.shape[1] // slab):
        mine, theirs = (v[:, i * slab : (i + 1) * slab] for v in (own, other))
        even = jnp.where(core_odd, theirs, mine)
        odd = jnp.where(core_odd, mine, theirs)
        both = jnp.concatenate([even, odd], axis=1)
        o_ref[:, 2 * i * slab : 2 * (i + 1) * slab] = both


def from_slabs(own, other, pos, slab):
    rows, cols = own.shape
    vmem = pl.BlockSpec(memory_space=pltpu.VMEM)
    return pl.pallas_call(
        functools.partial(from_slabs_kernel, slab=slab),
        in_specs=[pl.BlockSpec(memory_space=pltpu.SMEM), vmem, vmem],
        out_shape=jax.ShapeDtypeStruct((rows, 2 * cols), own.dtype),
        name="from_slabs",
    )(pos, own, other)


def assemble_kernel(pos_ref, *refs, block, nx, ny):
    o_ref = refs[-1]
    zi, xi, yi = pos_ref[0], pos_ref[2], pos_ref[3]
    rows = refs[0].shape[0]
    for n in range(nx // 2):
        for j in range(ny):
            ref = refs[n * ny + j]
            row = pl.multiple_of(((yi - j) & (ny - 1)) * rows, rows)
            for i in range(2):
                q = 2 * n + i
                for d, at in enumerate((zi * nx + ((xi - q) & (nx - 1)), (1 - zi) * nx + ((xi + q) & (nx - 1)))):
                    src = (2 * i + d) * block
                    o_ref[pl.ds(row, rows), pl.ds(pl.multiple_of(at * block, 128), block)] = ref[
                        :, src : src + block
                    ]


def assemble(pieces, pos, block, nx, ny):
    rows, cols = pieces[0].shape
    vmem = pl.BlockSpec(memory_space=pltpu.VMEM)
    return pl.pallas_call(
        functools.partial(assemble_kernel, block=block, nx=nx, ny=ny),
        in_specs=[pl.BlockSpec(memory_space=pltpu.SMEM)] + [vmem] * len(pieces),
        out_shape=jax.ShapeDtypeStruct((ny * rows, (nx // 2) * cols), pieces[0].dtype),
        name="assemble",
    )(pos, *pieces)


def layer(activations, grad_out, gate_pre, up_pre, gate_up, down_weight):
    tokens = activations.shape[0]
    slab, width = down_weight.shape
    nx, ny, nz = lax.axis_size(X), lax.axis_size(Y), lax.axis_size(ZH)
    dp_count = lax.axis_size(DP)
    rows = tokens // (ny * nz)
    xi, zi, ci = lax.axis_index(X), lax.axis_index(Z), lax.axis_index(C)
    yi = lax.axis_index(Y)
    pos = jnp.stack([zi, ci, xi, yi]).astype(jnp.int32)

    near, far = [down_weight], []
    far.append(swap(down_weight, Z))
    for _ in range(1, nx):
        near.append(ring(near[-1]))
        far.append(ring(far[-1]))
    gate_near = gate_up.reshape(slab, 2 * width)
    gate_far = [swap(gate_near, Z)]
    gate_near = [gate_near] + [None] * (nx - 1)
    gate_far = gate_far + [None] * (nx - 1)
    gate_near[1] = shift(gate_near[0], X, 1)
    gate_far[1] = shift(gate_far[0], X, -1)
    gate_near[3] = shift(gate_near[0], X, -1)
    gate_near[2] = shift(gate_near[1], X, 1)
    gate_far[3] = swap(gate_near[1], Z)
    gate_far[2] = swap(gate_near[2], Z)

    out_mine, out_theirs = to_columns(grad_out, pos, slab)
    out_theirs = swap(out_theirs, C)
    out_mine, _ = lax.optimization_barrier((out_mine, far[1]))
    out_all = jnp.concatenate([out_mine, out_theirs])
    both = jnp.concatenate([gate_pre.T, up_pre.T])
    other = swap(both, C)
    hidden, gate_factor, up_factor = factors(both, other)
    act_mine, act_theirs = to_columns(activations, pos, slab)
    act_theirs = swap(act_theirs, C)
    act_all = jnp.concatenate([act_mine, act_theirs])

    down = jnp.zeros((2 * nx, slab, width), BF)
    for h in range(nx):
        x = (xi + (2 * ci - 1) * h) & (nx - 1)
        down = lax.dynamic_update_slice(down, near[h][None], (zi * nx + x, 0, 0))
        down = lax.dynamic_update_slice(down, far[h][None], ((1 - zi) * nx + x, 0, 0))
    down = down.reshape(2 * nx * slab, width)
    part_h = lax.dot_general(down, out_all, (((0,), (1,)), ((), ())), preferred_element_type=F32)
    got_h = swap(part_h, C)
    grad_hidden = grad_hidden_of(part_h, got_h, gate_factor, up_factor)

    pieces = []
    for n in range(2):
        w = jnp.concatenate(
            [g[q] for q in (2 * n, 2 * n + 1) for g in (gate_near, gate_far)]
        )
        part = lax.dot_general(
            grad_hidden, w, (((0,), (1,)), ((), ())), preferred_element_type=F32
        ).astype(BF)
        if n == 0:
            part = part.reshape(2, ny * nz, rows, -1).transpose(1, 0, 2, 3)
            part = part.reshape(ny, 2 * nz * rows, -1)
            part = lax.all_to_all(part, Y, 0, 0, tiled=True)
            part = jnp.sum(part.astype(F32), axis=0)
        else:
            blocks = cut(part, pos, ny, nz, rows)
            part = blocks[0].astype(F32)
            for j in range(1, ny):
                got = shift(blocks[j], Y, j)
                part = part + got.astype(F32)
        part = part.astype(BF).reshape(nz, 2 * rows, -1)
        part = lax.all_to_all(part, ZH, 0, 0, tiled=True)
        part = jnp.sum(part.astype(F32), axis=0).astype(BF)
        got = swap(part[rows:], C)
        piece = from_slabs(part[:rows], got, pos, slab)
        piece = lax.all_gather(piece, ZH, axis=0, tiled=True)
        pieces.append(piece)
        for j in range(1, ny):
            pieces.append(shift(piece, Y, j))
    grad_input = assemble(pieces, pos, 2 * slab, nx, ny)

    grad_down = lax.dot_general(
        out_all, hidden, (((0,), (1,)), ((), ())), preferred_element_type=F32
    ).astype(BF)
    grad_down = lax.psum_scatter(grad_down, (Z, X), scatter_dimension=0, tiled=True)
    grad_down = grad_down.astype(F32) / dp_count
    total = lax.dot_general(
        act_all, grad_hidden, (((0,), (1,)), ((), ())), preferred_element_type=F32
    ).astype(BF)
    total = lax.psum_scatter(total, (Z, X), scatter_dimension=0, tiled=True)
    grad_gate_up = (total.astype(F32) / dp_count).reshape(slab, 2, width)
    return (grad_input, grad_gate_up, grad_down)


def solution(mesh):
    split = Mesh(
        mesh.devices.reshape(2, 4, 2, 4, 4), ("dp_0", "dp_1", "dp_2", "tensor_0", "tensor_1")
    )
    return jax.shard_map(
        layer,
        mesh=split,
        in_specs=(
            P(DP, None),
            P(DP, None),
            P(DP, TENSOR),
            P(DP, TENSOR),
            P(DP, None, TENSOR),
            P(DP, TENSOR),
        ),
        out_specs=(P(DP, None), P(DP, None, TENSOR), P(DP, TENSOR)),
        check_vma=False,
    )
```

profile of v0, /device:TPU:1, one launch (start us, length us, event | category | flops | bytes accessed | tf_op | source)
XLA Modules:
  0.0 334.1 jit_solution(16321565506205518784)
XLA Ops:
  7.8 5.0 %to_columns.2 = (bf16[256,2560]{1,0:T(8,128)(2,1)}, bf16[256,2560]{1,0:T(8,128)(2,1)}) custom-call(s32[4]{0:T(128)} %pad_add_fusion.pos_ref, bf16[256,5120]{1,0:T(8,128)(2,1)} %x_ref.2), custom_call_target="tpu_custom_call" | custom-call | tf_op jit(solution)/shard_map/to_columns/pallas_call | solution.py:52
  16.4 9.1 %collective-permute-done = bf16[320,448]{1,0:T(8,128)(2,1)} collective-permute-done((bf16[320,448]{1,0:T(8,128)(2,1)}, bf16[320,448]{1,0:T(8,128)(2,1)}, u32[]{:S(2)}, u32[]{:S(2)}) %collective-permute-start) | collective-permute-done | bytes 286752 | tf_op jit(solution)/shard_map/ppermute | solution.py:34
  38.9 5.0 %to_columns.3 = (bf16[256,2560]{1,0:T(8,128)(2,1)}, bf16[256,2560]{1,0:T(8,128)(2,1)}) custom-call(s32[4]{0:T(128)} %pad_add_fusion.pos_ref, bf16[256,5120]{1,0:T(8,128)(2,1)} %x_ref.3), custom_call_target="tpu_custom_call" | custom-call | tf_op jit(solution)/shard_map/to_columns/pallas_call | solution.py:52
  50.5 7.7 %collective-permute-done.3 = bf16[320,448]{1,0:T(8,128)(2,1)S(1)} collective-permute-done((bf16[320,448]{1,0:T(8,128)(2,1)S(1)}, bf16[320,448]{1,0:T(8,128)(2,1)S(1)}, u32[]{:S(2)}, u32[]{:S(2)}) %collective-permute-start.3) | collective-permute-done | bytes 286752 | tf_op jit(solution)/shard_map/ppermute | solution.py:30
  62.5 7.3 %collective-permute-done.4 = bf16[320,448]{1,0:T(8,128)(2,1)S(1)} collective-permute-done((bf16[320,448]{1,0:T(8,128)(2,1)}, bf16[320,448]{1,0:T(8,128)(2,1)S(1)}, u32[]{:S(2)}, u32[]{:S(2)}) %collective-permute-start.4) | collective-permute-done | bytes 286752 | tf_op jit(solution)/shard_map/ppermute | solution.py:30
  72.7 7.4 %collective-permute-done.5 = bf16[320,448]{1,0:T(8,128)(2,1)S(1)} collective-permute-done((bf16[320,448]{1,0:T(8,128)(2,1)S(1)}, bf16[320,448]{1,0:T(8,128)(2,1)S(1)}, u32[]{:S(2)}, u32[]{:S(2)}) %collective-permute-start.5) | collective-permute-done | bytes 286752 | tf_op jit(solution)/shard_map/ppermute | solution.py:30
  80.1 8.3 %collective-permute-done.6 = bf16[320,448]{1,0:T(8,128)(2,1)S(1)} collective-permute-done((bf16[320,448]{1,0:T(8,128)(2,1)S(1)}, bf16[320,448]{1,0:T(8,128)(2,1)S(1)}, u32[]{:S(2)}, u32[]{:S(2)}) %collective-permute-start.6) | collective-permute-done | bytes 286752 | tf_op jit(solution)/shard_map/ppermute | solution.py:30
  90.3 3.6 %collective-permute-start.8 = (f32[448,512]{1,0:T(8,128)S(1)}, f32[448,512]{1,0:T(8,128)S(1)}, u32[]{:S(2)}, u32[]{:S(2)}) collective-permute-start(f32[448,512]{1,0:T(8,128)S(1)} %fusion.25.part_ref), channel_id=1, source_target_pairs={{0,16},{16,0},{1,17},{17,1},{2,18},{18,2},{3,19},{19,3},{4,20},{20... | collective-permute-start | bytes 2752520 | tf_op jit(solution)/shard_map/ppermute | solution.py:34
  100.1 6.6 %convolution_convert_fusion = bf16[2560,896]{1,0:T(8,128)(2,1)} fusion(bf16[896,512]{1,0:T(8,128)(2,1)} %grad_hidden.1, bf16[256,2560]{1,0:T(8,128)(2,1)} %collective-permute-done.28, bf16[256,2560]{1,0:T(8,128)(2,1)S(1)} %copy-done.21), kind=kOutput, calls=%fused_computation | convolution fusion | flops 2356346880 | bytes 8126464 | tf_op jit(solution)/shard_map/dot_general | solution.py:259
  108.4 43.8 %collective-permute-done.11 = bf16[320,896]{1,0:T(8,128)(2,1)S(1)} collective-permute-done((bf16[320,896]{1,0:T(8,128)(2,1)S(1)}, bf16[320,896]{1,0:T(8,128)(2,1)S(1)}, u32[]{:S(2)}, u32[]{:S(2)}) %collective-permute-start.11) | collective-permute-done | bytes 573472 | tf_op jit(solution)/shard_map/ppermute | solution.py:21
  154.8 20.6 %collective-permute-done.17 = bf16[320,896]{1,0:T(8,128)(2,1)S(1)} collective-permute-done((bf16[320,896]{1,0:T(8,128)(2,1)S(1)}, bf16[320,896]{1,0:T(8,128)(2,1)S(1)}, u32[]{:S(2)}, u32[]{:S(2)}) %collective-permute-start.17) | collective-permute-done | bytes 573472 | tf_op jit(solution)/shard_map/ppermute | solution.py:21
  179.9 12.7 %collective-permute-done.18 = bf16[320,896]{1,0:T(8,128)(2,1)S(1)} collective-permute-done((bf16[320,896]{1,0:T(8,128)(2,1)S(1)}, bf16[320,896]{1,0:T(8,128)(2,1)S(1)}, u32[]{:S(2)}, u32[]{:S(2)}) %collective-permute-start.18) | collective-permute-done | bytes 573472 | tf_op jit(solution)/shard_map/ppermute | solution.py:34
  200.5 4.4 %collective-permute-done.10 = bf16[320,896]{1,0:T(8,128)(2,1)S(1)} collective-permute-done((bf16[320,896]{1,0:T(8,128)(2,1)S(1)}, bf16[320,896]{1,0:T(8,128)(2,1)S(1)}, u32[]{:S(2)}, u32[]{:S(2)}) %collective-permute-start.10) | collective-permute-done | bytes 573472 | tf_op jit(solution)/shard_map/ppermute | solution.py:34
  206.6 6.1 %collective-permute-done.22 = bf16[128,1280]{1,0:T(8,128)(2,1)S(1)} collective-permute-done((bf16[128,1280]{1,0:T(8,128)(2,1)}, bf16[128,1280]{1,0:T(8,128)(2,1)S(1)}, u32[]{:S(2)}, u32[]{:S(2)}) %collective-permute-start.22) | collective-permute-done | bytes 327712 | tf_op jit(solution)/shard_map/ppermute | solution.py:21
  216.8 5.8 %all-to-all-start.2 = ((bf16[4,32,1280]{2,1,0:T(8,128)(2,1)}), bf16[4,32,1280]{2,1,0:T(8,128)(2,1)S(1)}, u32[]{:S(2)}, u32[]{:S(2)}) async-start(bf16[4,32,1280]{2,1,0:T(8,128)(2,1)} %bitcast.24), calls=%async_computation.2 | async-start | bytes 655360 | tf_op jit(solution)/shard_map/all_to_all | solution.py:244
  225.4 5.6 %all-to-all-done.2 = bf16[4,32,1280]{2,1,0:T(8,128)(2,1)S(1)} async-done(((bf16[4,32,1280]{2,1,0:T(8,128)(2,1)}), bf16[4,32,1280]{2,1,0:T(8,128)(2,1)S(1)}, u32[]{:S(2)}, u32[]{:S(2)}) %all-to-all-start.2) | async-done | bytes 327712 | tf_op jit(solution)/shard_map/all_to_all | solution.py:244
  231.0 5.3 %all-to-all-start = ((bf16[4,128,1280]{2,1,0:T(8,128)(2,1)}), bf16[4,128,1280]{2,1,0:T(8,128)(2,1)S(1)}, u32[]{:S(2)}, u32[]{:S(2)}) async-start(bf16[4,128,1280]{2,1,0:T(8,128)(2,1)} %bitcast.17), calls=%async_computation | async-start | bytes 2621440 | tf_op jit(solution)/shard_map/all_to_all | solution.py:235
  236.4 14.1 %all-to-all-done = bf16[4,128,1280]{2,1,0:T(8,128)(2,1)S(1)} async-done(((bf16[4,128,1280]{2,1,0:T(8,128)(2,1)}), bf16[4,128,1280]{2,1,0:T(8,128)(2,1)S(1)}, u32[]{:S(2)}, u32[]{:S(2)}) %all-to-all-start) | async-done | bytes 1310752 | tf_op jit(solution)/shard_map/all_to_all | solution.py:235
  251.5 7.9 %all-to-all-start.1 = ((bf16[4,32,1280]{2,1,0:T(8,128)(2,1)}), bf16[4,32,1280]{2,1,0:T(8,128)(2,1)S(1)}, u32[]{:S(2)}, u32[]{:S(2)}) async-start(bf16[4,32,1280]{2,1,0:T(8,128)(2,1)} %bitcast.18), calls=%async_computation.1 | async-start | bytes 655360 | tf_op jit(solution)/shard_map/all_to_all | solution.py:244
  265.2 14.9 %all_gather.7.refs_4_ = bf16[64,2560]{1,0:T(8,128)(2,1)S(1)} all-gather(bf16[16,2560]{1,0:T(8,128)(2,1)} %from_slabs.3), channel_id=1, replica_groups=mesh['dp_0'=2,'dp_1'=4,'dp_2'=2,'tensor_0'=4,'tensor_1'=4] {'tensor_0'}, dimensions={0}, use_global_device_ids=true | all-gather | bytes 409600 | tf_op jit(solution)/shard_map/all_gather | solution.py:248
  289.3 12.1 %all_gather.6.refs_0_ = bf16[64,2560]{1,0:T(8,128)(2,1)S(1)} all-gather(bf16[16,2560]{1,0:T(8,128)(2,1)} %from_slabs.2), channel_id=1, replica_groups=mesh['dp_0'=2,'dp_1'=4,'dp_2'=2,'tensor_0'=4,'tensor_1'=4] {'tensor_0'}, dimensions={0}, use_global_device_ids=true | all-gather | bytes 409600 | tf_op jit(solution)/shard_map/all_gather | solution.py:248
  304.7 5.1 %collective-permute-done.14.refs_1_ = bf16[64,2560]{1,0:T(8,128)(2,1)S(1)} collective-permute-done((bf16[64,2560]{1,0:T(8,128)(2,1)S(1)}, bf16[64,2560]{1,0:T(8,128)(2,1)S(1)}, u32[]{:S(2)}, u32[]{:S(2)}) %collective-permute-start.14) | collective-permute-done | bytes 327712 | tf_op jit(solution)/shard_map/ppermute | solution.py:21
  309.7 5.5 %collective-permute-done.15.refs_2_ = bf16[64,2560]{1,0:T(8,128)(2,1)S(1)} collective-permute-done((bf16[64,2560]{1,0:T(8,128)(2,1)S(1)}, bf16[64,2560]{1,0:T(8,128)(2,1)S(1)}, u32[]{:S(2)}, u32[]{:S(2)}) %collective-permute-start.15) | collective-permute-done | bytes 327712 | tf_op jit(solution)/shard_map/ppermute | solution.py:21
  318.5 3.4 %assemble.1 = bf16[256,5120]{1,0:T(8,128)(2,1)} custom-call(s32[4]{0:T(128)} %pad_add_fusion.pos_ref, bf16[64,2560]{1,0:T(8,128)(2,1)} %copy-done.3, bf16[64,2560]{1,0:T(8,128)(2,1)} %copy-done.14, bf16[64,2560]{1,0:T(8,128)(2,1)} %copy-done.15, bf16[64,2560]{1,0:T(8,128)(2,1)} %copy-done.16, bf16[64,2560]{1,0:T(8,128)(2,1)} %copy-done.2, ...), custom_call_target="tpu_custom_call" | custom-call | tf_op jit(solution)/shard_map/assemble/pallas_call | solution.py:169
  (131 shorter events, 92.4 us)
Async XLA Ops:
  7.2 314.7 %reduce-scatter.5.cloned.1.call-start = ((), (), s32[]{:S(2)}) async-start(), calls=%async_computation.6 | async-start | bytes 2949120 | tf_op jit(solution)/shard_map/reduce_scatter | solution.py:257
  12.8 19.3 %collective-permute-start.7 = (bf16[256,2560]{1,0:T(8,128)(2,1)}, bf16[256,2560]{1,0:T(8,128)(2,1)S(1)}, u32[]{:S(2)}, u32[]{:S(2)}) collective-permute-start(bf16[256,2560]{1,0:T(8,128)(2,1)} %get-tuple-element.17), channel_id=1, source_target_pairs={{0,16},{16,0},{1,17},{17,1},{2,18},{18,2},{3,19},{19,3},{4,20},{20... | collective-permute-start | bytes 3932168 | tf_op jit(solution)/shard_map/ppermute | solution.py:34
  36.8 287.0 %reduce-scatter.3.cloned.1.call-start = ((), (), s32[]{:S(2)}) async-start(), calls=%async_computation.5 | async-start | bytes 5160960 | tf_op jit(solution)/shard_map/reduce_scatter | solution.py:262
  43.9 56.2 %collective-permute-start.28 = (bf16[256,2560]{1,0:T(8,128)(2,1)}, bf16[256,2560]{1,0:T(8,128)(2,1)}, u32[]{:S(2)}, u32[]{:S(2)}) collective-permute-start(bf16[256,2560]{1,0:T(8,128)(2,1)} %get-tuple-element.25), channel_id=1, source_target_pairs={{0,16},{16,0},{1,17},{17,1},{2,18},{18,2},{3,19},{19,3},{4,20},{20... | collective-permute-start | bytes 3932168 | tf_op jit(solution)/shard_map/ppermute | solution.py:34
  50.4 19.4 %collective-permute-start.4 = (bf16[320,448]{1,0:T(8,128)(2,1)}, bf16[320,448]{1,0:T(8,128)(2,1)S(1)}, u32[]{:S(2)}, u32[]{:S(2)}) collective-permute-start(bf16[320,448]{1,0:T(8,128)(2,1)} %collective-permute-done.2), channel_id=1, source_target_pairs={{0,32},{16,112},{32,64},{48,16},{64,96},{80,48},{96,0},{112,80},{1... | collective-permute-start | bytes 860168 | tf_op jit(solution)/shard_map/ppermute | solution.py:30
  58.2 21.9 %collective-permute-start.5 = (bf16[320,448]{1,0:T(8,128)(2,1)S(1)}, bf16[320,448]{1,0:T(8,128)(2,1)S(1)}, u32[]{:S(2)}, u32[]{:S(2)}) collective-permute-start(bf16[320,448]{1,0:T(8,128)(2,1)S(1)} %collective-permute-done.3), channel_id=1, source_target_pairs={{0,32},{16,112},{32,64},{48,16},{64,96},{80,48},{96,0},{112,80},{1... | collective-permute-start | bytes 860168 | tf_op jit(solution)/shard_map/ppermute | solution.py:30
  69.7 18.7 %collective-permute-start.6 = (bf16[320,448]{1,0:T(8,128)(2,1)S(1)}, bf16[320,448]{1,0:T(8,128)(2,1)S(1)}, u32[]{:S(2)}, u32[]{:S(2)}) collective-permute-start(bf16[320,448]{1,0:T(8,128)(2,1)S(1)} %collective-permute-done.4), channel_id=1, source_target_pairs={{0,32},{16,112},{32,64},{48,16},{64,96},{80,48},{96,0},{112,80},{1... | collective-permute-start | bytes 860168 | tf_op jit(solution)/shard_map/ppermute | solution.py:30
  108.3 43.9 %collective-permute-start.11 = (bf16[320,896]{1,0:T(8,128)(2,1)S(1)}, bf16[320,896]{1,0:T(8,128)(2,1)S(1)}, u32[]{:S(2)}, u32[]{:S(2)}) collective-permute-start(bf16[320,896]{1,0:T(8,128)(2,1)S(1)} %reshape.43), channel_id=1, source_target_pairs={{0,32},{32,64},{64,96},{96,0},{1,33},{33,65},{65,97},{97,1},{2,34}... | collective-permute-start | bytes 1720328 | tf_op jit(solution)/shard_map/ppermute | solution.py:21
  152.1 23.3 %collective-permute-start.17 = (bf16[320,896]{1,0:T(8,128)(2,1)S(1)}, bf16[320,896]{1,0:T(8,128)(2,1)S(1)}, u32[]{:S(2)}, u32[]{:S(2)}) collective-permute-start(bf16[320,896]{1,0:T(8,128)(2,1)S(1)} %collective-permute-done.11), channel_id=1, source_target_pairs={{0,32},{32,64},{64,96},{96,0},{1,33},{33,65},{65,97},{97,1},{2,34}... | collective-permute-start | bytes 1720328 | tf_op jit(solution)/shard_map/ppermute | solution.py:21
  152.1 25.1 %collective-permute-start.19 = (bf16[320,896]{1,0:T(8,128)(2,1)S(1)}, bf16[320,896]{1,0:T(8,128)(2,1)S(1)}, u32[]{:S(2)}, u32[]{:S(2)}) collective-permute-start(bf16[320,896]{1,0:T(8,128)(2,1)S(1)} %reshape.43), channel_id=1, source_target_pairs={{0,96},{32,0},{64,32},{96,64},{1,97},{33,1},{65,33},{97,65},{2,98}... | collective-permute-start | bytes 1720328 | tf_op jit(solution)/shard_map/ppermute | solution.py:21
  154.8 25.1 %collective-permute-start.20 = (bf16[320,896]{1,0:T(8,128)(2,1)S(1)}, bf16[320,896]{1,0:T(8,128)(2,1)S(1)}, u32[]{:S(2)}, u32[]{:S(2)}) collective-permute-start(bf16[320,896]{1,0:T(8,128)(2,1)S(1)} %collective-permute-done.11), channel_id=1, source_target_pairs={{0,128},{128,0},{1,129},{129,1},{2,130},{130,2},{3,131},{131,3},{4... | collective-permute-start | bytes 1720328 | tf_op jit(solution)/shard_map/ppermute | solution.py:34
  175.5 17.2 %collective-permute-start.18 = (bf16[320,896]{1,0:T(8,128)(2,1)S(1)}, bf16[320,896]{1,0:T(8,128)(2,1)S(1)}, u32[]{:S(2)}, u32[]{:S(2)}) collective-permute-start(bf16[320,896]{1,0:T(8,128)(2,1)S(1)} %collective-permute-done.17), channel_id=1, source_target_pairs={{0,128},{128,0},{1,129},{129,1},{2,130},{130,2},{3,131},{131,3},{4... | collective-permute-start | bytes 1720328 | tf_op jit(solution)/shard_map/ppermute | solution.py:34
  175.5 29.5 %collective-permute-start.10 = (bf16[320,896]{1,0:T(8,128)(2,1)S(1)}, bf16[320,896]{1,0:T(8,128)(2,1)S(1)}, u32[]{:S(2)}, u32[]{:S(2)}) collective-permute-start(bf16[320,896]{1,0:T(8,128)(2,1)S(1)} %reshape.43), channel_id=1, source_target_pairs={{0,128},{128,0},{1,129},{129,1},{2,130},{130,2},{3,131},{131,3},{4... | collective-permute-start | bytes 1720328 | tf_op jit(solution)/shard_map/ppermute | solution.py:34
  197.8 14.9 %collective-permute-start.22 = (bf16[128,1280]{1,0:T(8,128)(2,1)}, bf16[128,1280]{1,0:T(8,128)(2,1)S(1)}, u32[]{:S(2)}, u32[]{:S(2)}) collective-permute-start(bf16[128,1280]{1,0:T(8,128)(2,1)} %bitcast.49), channel_id=1, source_target_pairs={{0,2},{1,3},{2,0},{3,1},{4,6},{5,7},{6,4},{7,5},{8,10},{9,11},{10,... | collective-permute-start | bytes 983048 | tf_op jit(solution)/shard_map/ppermute | solution.py:21
  200.1 14.9 %collective-permute-start.23 = (bf16[128,1280]{1,0:T(8,128)(2,1)}, bf16[128,1280]{1,0:T(8,128)(2,1)S(1)}, u32[]{:S(2)}, u32[]{:S(2)}) collective-permute-start(bf16[128,1280]{1,0:T(8,128)(2,1)} %bitcast.48), channel_id=1, source_target_pairs={{0,3},{1,0},{2,1},{3,2},{4,7},{5,4},{6,5},{7,6},{8,11},{9,8},{10,9... | collective-permute-start | bytes 983048 | tf_op jit(solution)/shard_map/ppermute | solution.py:21
  204.9 17.7 %collective-permute-start.12 = (bf16[320,896]{1,0:T(8,128)(2,1)S(1)}, bf16[320,896]{1,0:T(8,128)(2,1)S(1)}, u32[]{:S(2)}, u32[]{:S(2)}) collective-permute-start(bf16[320,896]{1,0:T(8,128)(2,1)S(1)} %collective-permute-done.10), channel_id=1, source_target_pairs={{0,96},{32,0},{64,32},{96,64},{1,97},{33,1},{65,33},{97,65},{2,98}... | collective-permute-start | bytes 1720328 | tf_op jit(solution)/shard_map/ppermute | solution.py:21
  216.8 14.2 %all-to-all-start.2 = ((bf16[4,32,1280]{2,1,0:T(8,128)(2,1)}), bf16[4,32,1280]{2,1,0:T(8,128)(2,1)S(1)}, u32[]{:S(2)}, u32[]{:S(2)}) async-start(bf16[4,32,1280]{2,1,0:T(8,128)(2,1)} %bitcast.24), calls=%async_computation.2 | async-start | bytes 655360 | tf_op jit(solution)/shard_map/all_to_all | solution.py:244
  231.0 19.4 %all-to-all-start = ((bf16[4,128,1280]{2,1,0:T(8,128)(2,1)}), bf16[4,128,1280]{2,1,0:T(8,128)(2,1)S(1)}, u32[]{:S(2)}, u32[]{:S(2)}) async-start(bf16[4,128,1280]{2,1,0:T(8,128)(2,1)} %bitcast.17), calls=%async_computation | async-start | bytes 2621440 | tf_op jit(solution)/shard_map/all_to_all | solution.py:235
  251.5 29.0 %all-to-all-start.1 = ((bf16[4,32,1280]{2,1,0:T(8,128)(2,1)}), bf16[4,32,1280]{2,1,0:T(8,128)(2,1)S(1)}, u32[]{:S(2)}, u32[]{:S(2)}) async-start(bf16[4,32,1280]{2,1,0:T(8,128)(2,1)} %bitcast.18), calls=%async_computation.1 | async-start | bytes 655360 | tf_op jit(solution)/shard_map/all_to_all | solution.py:244
  280.2 23.2 %collective-permute-start.25 = (bf16[64,2560]{1,0:T(8,128)(2,1)S(1)}, bf16[64,2560]{1,0:T(8,128)(2,1)S(1)}, u32[]{:S(2)}, u32[]{:S(2)}) collective-permute-start(bf16[64,2560]{1,0:T(8,128)(2,1)S(1)} %all_gather.7.refs_4_), channel_id=1, source_target_pairs={{0,1},{1,2},{2,3},{3,0},{4,5},{5,6},{6,7},{7,4},{8,9},{9,10},{10,1... | collective-permute-start | bytes 983048 | tf_op jit(solution)/shard_map/ppermute | solution.py:21
  283.8 20.9 %collective-permute-start.26 = (bf16[64,2560]{1,0:T(8,128)(2,1)S(1)}, bf16[64,2560]{1,0:T(8,128)(2,1)S(1)}, u32[]{:S(2)}, u32[]{:S(2)}) collective-permute-start(bf16[64,2560]{1,0:T(8,128)(2,1)S(1)} %all_gather.7.refs_4_), channel_id=1, source_target_pairs={{0,2},{1,3},{2,0},{3,1},{4,6},{5,7},{6,4},{7,5},{8,10},{9,11},{10,... | collective-permute-start | bytes 983048 | tf_op jit(solution)/shard_map/ppermute | solution.py:21
  286.2 18.5 %collective-permute-start.27 = (bf16[64,2560]{1,0:T(8,128)(2,1)S(1)}, bf16[64,2560]{1,0:T(8,128)(2,1)S(1)}, u32[]{:S(2)}, u32[]{:S(2)}) collective-permute-start(bf16[64,2560]{1,0:T(8,128)(2,1)S(1)} %all_gather.7.refs_4_), channel_id=1, source_target_pairs={{0,3},{1,0},{2,1},{3,2},{4,7},{5,4},{6,5},{7,6},{8,11},{9,8},{10,9... | collective-permute-start | bytes 983048 | tf_op jit(solution)/shard_map/ppermute | solution.py:21
  302.1 13.1 %collective-permute-start.15 = (bf16[64,2560]{1,0:T(8,128)(2,1)S(1)}, bf16[64,2560]{1,0:T(8,128)(2,1)S(1)}, u32[]{:S(2)}, u32[]{:S(2)}) collective-permute-start(bf16[64,2560]{1,0:T(8,128)(2,1)S(1)} %all_gather.6.refs_0_), channel_id=1, source_target_pairs={{0,2},{1,3},{2,0},{3,1},{4,6},{5,7},{6,4},{7,5},{8,10},{9,11},{10,... | collective-permute-start | bytes 983048 | tf_op jit(solution)/shard_map/ppermute | solution.py:21
  303.4 14.4 %collective-permute-start.16 = (bf16[64,2560]{1,0:T(8,128)(2,1)S(1)}, bf16[64,2560]{1,0:T(8,128)(2,1)S(1)}, u32[]{:S(2)}, u32[]{:S(2)}) collective-permute-start(bf16[64,2560]{1,0:T(8,128)(2,1)S(1)} %all_gather.6.refs_0_), channel_id=1, source_target_pairs={{0,3},{1,0},{2,1},{3,2},{4,7},{5,4},{6,5},{7,6},{8,11},{9,8},{10,9... | collective-permute-start | bytes 983048 | tf_op jit(solution)/shard_map/ppermute | solution.py:21
  (33 other events, 385.0 us)
Sparse Core Ops, SparseCore 0:
  36.9 52.6 reduce-scatter.4
  106.8 77.6 reduce-scatter.2
where the time goes:
time: 336 us; the launch traced here: 334 us
  waiting for transfers between devices  170 us (51%)
  starting transfers between devices  59.9 us (18%)
  blocking collectives  27.1 us (8%)
  Pallas kernels  25 us (7%)
  matrix products  15.7 us (5%)
  local copies, waits for them, and re-layouts  15.2 us (5%)
  between operations  14.3 us (4%)
  other arithmetic  6.56 us (2%)
    ppermute x13, waiting for transfers between devices, shift(): return lax.ppermute(v, axis, [(i, (i + step) % n) for i in range(n)])  86.4 us
    ppermute x6, waiting for transfers between devices, ring(): return lax.ppermute(v, (X, C), pairs)  32.4 us
    ppermute x10, waiting for transfers between devices, swap(): return lax.ppermute(v, axis, [(0, 1), (1, 0)])  31.8 us
    all_gather x2, blocking collectives, layer(): piece = lax.all_gather(piece, ZH, axis=0, tiled=True)  27.1 us
    ppermute x10, starting transfers between devices, swap(): return lax.ppermute(v, axis, [(0, 1), (1, 0)])  14.4 us
    all_to_all x1, waiting for transfers between devices, layer(): part = lax.all_to_all(part, Y, 0, 0, tiled=True)  14.1 us
    all_to_all x2, starting transfers between devices, layer(): part = lax.all_to_all(part, ZH, 0, 0, tiled=True)  13.8 us
    ppermute x13, starting transfers between devices, shift(): return lax.ppermute(v, axis, [(i, (i + step) % n) for i in range(n)])  13.7 us
  transfers between devices with their start and end apart: 34, of which 22 were waited for; matrix products, arithmetic and copies ran while one was open for 7% of the time, Pallas kernels for 6%

commit v1 on v0

--- a/solution.py
+++ b/solution.py
@@ -19,15 +19,6 @@
 def shift(v, axis, step):
     n = lax.axis_size(axis)
     return lax.ppermute(v, axis, [(i, (i + step) % n) for i in range(n)])
-
-
-def ring(v):
-    n = lax.axis_size(X)
-    pairs = []
-    for i in range(n):
-        pairs.append((2 * i, 2 * ((i + 1) % n)))
-        pairs.append((2 * i + 1, 2 * ((i - 1) % n) + 1))
-    return lax.ppermute(v, (X, C), pairs)
 
 
 def swap(v, axis):
@@ -184,11 +175,14 @@
     yi = lax.axis_index(Y)
     pos = jnp.stack([zi, ci, xi, yi]).astype(jnp.int32)
 
-    near, far = [down_weight], []
-    far.append(swap(down_weight, Z))
-    for _ in range(1, nx):
-        near.append(ring(near[-1]))
-        far.append(ring(far[-1]))
+    near, far = [down_weight] + [None] * (nx - 1), [None] * nx
+    far[0] = swap(down_weight, Z)
+    near[1] = shift(near[0], X, 1)
+    near[3] = shift(near[0], X, -1)
+    far[1] = shift(far[0], X, -1)
+    far[3] = shift(far[0], X, 1)
+    near[2] = shift(near[1], X, 1)
+    far[2] = shift(far[1], X, -1)
     gate_near = gate_up.reshape(slab, 2 * width)
     gate_far = [swap(gate_near, Z)]
     gate_near = [gate_near] + [None] * (nx - 1)
@@ -212,9 +206,10 @@
     act_all = jnp.concatenate([act_mine, act_theirs])
 
     down = jnp.zeros((2 * nx, slab, width), BF)
-    for h in range(nx):
-        x = (xi + (2 * ci - 1) * h) & (nx - 1)
+    for h in (0, 1, 3, 2):
+        x = (xi - h) & (nx - 1)
         down = lax.dynamic_update_slice(down, near[h][None], (zi * nx + x, 0, 0))
+        x = (xi + h) & (nx - 1)
         down = lax.dynamic_update_slice(down, far[h][None], ((1 - zi) * nx + x, 0, 0))
     down = down.reshape(2 * nx * slab, width)
     part_h = lax.dot_general(down, out_all, (((0,), (1,)), ((), ())), preferred_element_type=F32)

time: 336 us -> 334 us (level)
    ppermute x6 -> x0, waiting for transfers between devices: 32.4 us -> none  [ring(): return lax.ppermute(v, (X, C), pairs)]
    ppermute x13 -> x19, waiting for transfers between devices: 86.4 us -> 112 us  [shift(): return lax.ppermute(v, axis, [(i, (i + step) % n) for i in range(n)])]
    ppermute x6 -> x0, starting transfers between devices: 12.6 us -> none  [ring(): return lax.ppermute(v, (X, C), pairs)]
    ppermute x10, starting transfers between devices: 14.4 us -> 24.2 us  [swap(): return lax.ppermute(v, axis, [(0, 1), (1, 0)])]
    ppermute x13 -> x19, starting transfers between devices: 13.7 us -> 20 us  [shift(): return lax.ppermute(v, axis, [(i, (i + step) % n) for i in range(n)])]
    all_to_all x2, starting transfers between devices: 13.8 us -> 9.34 us  [layer(): part = lax.all_to_all(part, ZH, 0, 0, tiled=True)]
  transfers between devices with their start and end apart: 34 -> 34, of which waited for: 22 -> 16; matrix products, arithmetic and copies ran while one was open for 7% -> 7% of each run, Pallas kernels for 6% -> 6%
where the time goes in v1:
time: 334 us; the launch traced here: 330 us
  waiting for transfers between devices  167 us (50%)
  starting transfers between devices  59.1 us (18%)
  blocking collectives  27.2 us (8%)
  Pallas kernels  25 us (7%)
  matrix products  15.6 us (5%)
  local copies, waits for them, and re-layouts  15.2 us (5%)
  between operations  14.4 us (4%)
  other arithmetic  6.56 us (2%)
    ppermute x19, waiting for transfers between devices, shift(): return lax.ppermute(v, axis, [(i, (i + step) % n) for i in range(n)])  112 us
    ppermute x10, waiting for transfers between devices, swap(): return lax.ppermute(v, axis, [(0, 1), (1, 0)])  35.1 us
    all_gather x2, blocking collectives, layer(): piece = lax.all_gather(piece, ZH, axis=0, tiled=True)  27.2 us
    ppermute x10, starting transfers between devices, swap(): return lax.ppermute(v, axis, [(0, 1), (1, 0)])  24.2 us
    ppermute x19, starting transfers between devices, shift(): return lax.ppermute(v, axis, [(i, (i + step) % n) for i in range(n)])  20 us
    all_to_all x1, waiting for transfers between devices, layer(): part = lax.all_to_all(part, Y, 0, 0, tiled=True)  13.6 us
    pallas_call x2, Pallas kernels, to_columns(): pl.pallas_call(functools.partial(to_columns_kernel, slab=slab), grid_spec...  9.92 us
    all_to_all x2, starting transfers between devices, layer(): part = lax.all_to_all(part, ZH, 0, 0, tiled=True)  9.34 us
  transfers between devices with their start and end apart: 34, of which 16 were waited for; matrix products, arithmetic and copies ran while one was open for 7% of the time, Pallas kernels for 6%

profile of v1, /device:TPU:1, one launch (start us, length us, event | category | flops | bytes accessed | tf_op | source)
XLA Modules:
  0.0 330.3 jit_solution(7287407852616201838)
XLA Ops:
  7.8 5.0 %to_columns.2 = (bf16[256,2560]{1,0:T(8,128)(2,1)}, bf16[256,2560]{1,0:T(8,128)(2,1)}) custom-call(s32[4]{0:T(128)} %pad_add_fusion.pos_ref, bf16[256,5120]{1,0:T(8,128)(2,1)} %x_ref.2), custom_call_target="tpu_custom_call" | custom-call | tf_op jit(solution)/shard_map/to_columns/pallas_call | solution.py:43
  16.4 9.1 %collective-permute-done = bf16[320,448]{1,0:T(8,128)(2,1)} collective-permute-done((bf16[320,448]{1,0:T(8,128)(2,1)}, bf16[320,448]{1,0:T(8,128)(2,1)}, u32[]{:S(2)}, u32[]{:S(2)}) %collective-permute-start) | collective-permute-done | bytes 286752 | tf_op jit(solution)/shard_map/ppermute | solution.py:25
  30.3 3.8 %collective-permute-done.2 = bf16[320,448]{1,0:T(8,128)(2,1)} collective-permute-done((bf16[320,448]{1,0:T(8,128)(2,1)}, bf16[320,448]{1,0:T(8,128)(2,1)}, u32[]{:S(2)}, u32[]{:S(2)}) %collective-permute-start.2) | collective-permute-done | bytes 286752 | tf_op jit(solution)/shard_map/ppermute | solution.py:21
  41.7 5.0 %to_columns.3 = (bf16[256,2560]{1,0:T(8,128)(2,1)}, bf16[256,2560]{1,0:T(8,128)(2,1)}) custom-call(s32[4]{0:T(128)} %pad_add_fusion.pos_ref, bf16[256,5120]{1,0:T(8,128)(2,1)} %x_ref.3), custom_call_target="tpu_custom_call" | custom-call | tf_op jit(solution)/shard_map/to_columns/pallas_call | solution.py:43
  55.5 12.3 %collective-permute-done.4 = bf16[320,448]{1,0:T(8,128)(2,1)S(1)} collective-permute-done((bf16[320,448]{1,0:T(8,128)(2,1)}, bf16[320,448]{1,0:T(8,128)(2,1)S(1)}, u32[]{:S(2)}, u32[]{:S(2)}) %collective-permute-start.4) | collective-permute-done | bytes 286752 | tf_op jit(solution)/shard_map/ppermute | solution.py:21
  67.8 14.5 %collective-permute-done.5 = bf16[320,448]{1,0:T(8,128)(2,1)S(1)} collective-permute-done((bf16[320,448]{1,0:T(8,128)(2,1)S(1)}, bf16[320,448]{1,0:T(8,128)(2,1)S(1)}, u32[]{:S(2)}, u32[]{:S(2)}) %collective-permute-start.5) | collective-permute-done | bytes 286752 | tf_op jit(solution)/shard_map/ppermute | solution.py:21
  84.1 6.8 %collective-permute-start.8 = (f32[448,512]{1,0:T(8,128)S(1)}, f32[448,512]{1,0:T(8,128)S(1)}, u32[]{:S(2)}, u32[]{:S(2)}) collective-permute-start(f32[448,512]{1,0:T(8,128)S(1)} %fusion.25.part_ref), channel_id=1, source_target_pairs={{0,16},{16,0},{1,17},{17,1},{2,18},{18,2},{3,19},{19,3},{4,20},{20... | collective-permute-start | bytes 2752520 | tf_op jit(solution)/shard_map/ppermute | solution.py:25
  97.1 6.6 %convolution_convert_fusion = bf16[2560,896]{1,0:T(8,128)(2,1)} fusion(bf16[896,512]{1,0:T(8,128)(2,1)} %grad_hidden.1, bf16[256,2560]{1,0:T(8,128)(2,1)} %collective-permute-done.28, bf16[256,2560]{1,0:T(8,128)(2,1)S(1)} %copy-done.21), kind=kOutput, calls=%fused_computation | convolution fusion | flops 2356346880 | bytes 8126464 | tf_op jit(solution)/shard_map/dot_general | solution.py:254
  105.4 39.1 %collective-permute-done.11 = bf16[320,896]{1,0:T(8,128)(2,1)S(1)} collective-permute-done((bf16[320,896]{1,0:T(8,128)(2,1)S(1)}, bf16[320,896]{1,0:T(8,128)(2,1)S(1)}, u32[]{:S(2)}, u32[]{:S(2)}) %collective-permute-start.11) | collective-permute-done | bytes 573472 | tf_op jit(solution)/shard_map/ppermute | solution.py:21
  147.2 20.3 %collective-permute-done.17 = bf16[320,896]{1,0:T(8,128)(2,1)S(1)} collective-permute-done((bf16[320,896]{1,0:T(8,128)(2,1)S(1)}, bf16[320,896]{1,0:T(8,128)(2,1)S(1)}, u32[]{:S(2)}, u32[]{:S(2)}) %collective-permute-start.17) | collective-permute-done | bytes 573472 | tf_op jit(solution)/shard_map/ppermute | solution.py:21
  167.5 3.9 %collective-permute-start.18 = (bf16[320,896]{1,0:T(8,128)(2,1)S(1)}, bf16[320,896]{1,0:T(8,128)(2,1)S(1)}, u32[]{:S(2)}, u32[]{:S(2)}) collective-permute-start(bf16[320,896]{1,0:T(8,128)(2,1)S(1)} %collective-permute-done.17), channel_id=1, source_target_pairs={{0,128},{128,0},{1,129},{129,1},{2,130},{130,2},{3,131},{131,3},{4... | collective-permute-start | bytes 1720328 | tf_op jit(solution)/shard_map/ppermute | solution.py:25
  171.4 18.6 %collective-permute-done.18 = bf16[320,896]{1,0:T(8,128)(2,1)S(1)} collective-permute-done((bf16[320,896]{1,0:T(8,128)(2,1)S(1)}, bf16[320,896]{1,0:T(8,128)(2,1)S(1)}, u32[]{:S(2)}, u32[]{:S(2)}) %collective-permute-start.18) | collective-permute-done | bytes 573472 | tf_op jit(solution)/shard_map/ppermute | solution.py:25
  197.9 4.5 %collective-permute-done.10 = bf16[320,896]{1,0:T(8,128)(2,1)S(1)} collective-permute-done((bf16[320,896]{1,0:T(8,128)(2,1)S(1)}, bf16[320,896]{1,0:T(8,128)(2,1)S(1)}, u32[]{:S(2)}, u32[]{:S(2)}) %collective-permute-start.10) | collective-permute-done | bytes 573472 | tf_op jit(solution)/shard_map/ppermute | solution.py:25
  203.4 9.5 %collective-permute-done.21 = bf16[128,1280]{1,0:T(8,128)(2,1)S(1)} collective-permute-done((bf16[128,1280]{1,0:T(8,128)(2,1)}, bf16[128,1280]{1,0:T(8,128)(2,1)S(1)}, u32[]{:S(2)}, u32[]{:S(2)}) %collective-permute-start.21) | collective-permute-done | bytes 327712 | tf_op jit(solution)/shard_map/ppermute | solution.py:21
  214.8 4.7 %all-to-all-start.2 = ((bf16[4,32,1280]{2,1,0:T(8,128)(2,1)}), bf16[4,32,1280]{2,1,0:T(8,128)(2,1)S(1)}, u32[]{:S(2)}, u32[]{:S(2)}) async-start(bf16[4,32,1280]{2,1,0:T(8,128)(2,1)} %bitcast.24), calls=%async_computation.2 | async-start | bytes 655360 | tf_op jit(solution)/shard_map/all_to_all | solution.py:239
  222.2 6.4 %all-to-all-done.2 = bf16[4,32,1280]{2,1,0:T(8,128)(2,1)S(1)} async-done(((bf16[4,32,1280]{2,1,0:T(8,128)(2,1)}), bf16[4,32,1280]{2,1,0:T(8,128)(2,1)S(1)}, u32[]{:S(2)}, u32[]{:S(2)}) %all-to-all-start.2) | async-done | bytes 327712 | tf_op jit(solution)/shard_map/all_to_all | solution.py:239
  228.6 5.5 %all-to-all-start = ((bf16[4,128,1280]{2,1,0:T(8,128)(2,1)}), bf16[4,128,1280]{2,1,0:T(8,128)(2,1)S(1)}, u32[]{:S(2)}, u32[]{:S(2)}) async-start(bf16[4,128,1280]{2,1,0:T(8,128)(2,1)} %bitcast.17), calls=%async_computation | async-start | bytes 2621440 | tf_op jit(solution)/shard_map/all_to_all | solution.py:230
  234.2 13.6 %all-to-all-done = bf16[4,128,1280]{2,1,0:T(8,128)(2,1)S(1)} async-done(((bf16[4,128,1280]{2,1,0:T(8,128)(2,1)}), bf16[4,128,1280]{2,1,0:T(8,128)(2,1)S(1)}, u32[]{:S(2)}, u32[]{:S(2)}) %all-to-all-start) | async-done | bytes 1310752 | tf_op jit(solution)/shard_map/all_to_all | solution.py:230
  248.8 4.6 %all-to-all-start.1 = ((bf16[4,32,1280]{2,1,0:T(8,128)(2,1)}), bf16[4,32,1280]{2,1,0:T(8,128)(2,1)S(1)}, u32[]{:S(2)}, u32[]{:S(2)}) async-start(bf16[4,32,1280]{2,1,0:T(8,128)(2,1)} %bitcast.18), calls=%async_computation.1 | async-start | bytes 655360 | tf_op jit(solution)/shard_map/all_to_all | solution.py:239
  254.0 4.0 %collective-permute-start.24 = (bf16[16,1280]{1,0:T(8,128)(2,1)S(1)}, bf16[16,1280]{1,0:T(8,128)(2,1)S(1)}, u32[]{:S(2)}, u32[]{:S(2)}) collective-permute-start(bf16[16,1280]{1,0:T(8,128)(2,1)S(1)} %get-tuple-element.27), channel_id=1, source_target_pairs={{0,16},{16,0},{1,17},{17,1},{2,18},{18,2},{3,19},{19,3},{4,20},{20... | collective-permute-start | bytes 122888 | tf_op jit(solution)/shard_map/ppermute | solution.py:25
  261.2 14.8 %all_gather.7.refs_4_ = bf16[64,2560]{1,0:T(8,128)(2,1)S(1)} all-gather(bf16[16,2560]{1,0:T(8,128)(2,1)} %from_slabs.3), channel_id=1, replica_groups=mesh['dp_0'=2,'dp_1'=4,'dp_2'=2,'tensor_0'=4,'tensor_1'=4] {'tensor_0'}, dimensions={0}, use_global_device_ids=true | all-gather | bytes 409600 | tf_op jit(solution)/shard_map/all_gather | solution.py:243
  285.0 12.4 %all_gather.6.refs_0_ = bf16[64,2560]{1,0:T(8,128)(2,1)S(1)} all-gather(bf16[16,2560]{1,0:T(8,128)(2,1)} %from_slabs.2), channel_id=1, replica_groups=mesh['dp_0'=2,'dp_1'=4,'dp_2'=2,'tensor_0'=4,'tensor_1'=4] {'tensor_0'}, dimensions={0}, use_global_device_ids=true | all-gather | bytes 409600 | tf_op jit(solution)/shard_map/all_gather | solution.py:243
  301.6 3.8 %collective-permute-done.14.refs_1_ = bf16[64,2560]{1,0:T(8,128)(2,1)S(1)} collective-permute-done((bf16[64,2560]{1,0:T(8,128)(2,1)S(1)}, bf16[64,2560]{1,0:T(8,128)(2,1)S(1)}, u32[]{:S(2)}, u32[]{:S(2)}) %collective-permute-start.14) | collective-permute-done | bytes 327712 | tf_op jit(solution)/shard_map/ppermute | solution.py:21
  305.4 6.4 %collective-permute-done.15.refs_2_ = bf16[64,2560]{1,0:T(8,128)(2,1)S(1)} collective-permute-done((bf16[64,2560]{1,0:T(8,128)(2,1)S(1)}, bf16[64,2560]{1,0:T(8,128)(2,1)S(1)}, u32[]{:S(2)}, u32[]{:S(2)}) %collective-permute-start.15) | collective-permute-done | bytes 327712 | tf_op jit(solution)/shard_map/ppermute | solution.py:21
  (131 shorter events, 80.7 us)
Async XLA Ops:
  7.2 311.0 %reduce-scatter.5.cloned.1.call-start = ((), (), s32[]{:S(2)}) async-start(), calls=%async_computation.6 | async-start | bytes 2949120 | tf_op jit(solution)/shard_map/reduce_scatter | solution.py:252
  12.8 21.4 %collective-permute-start.7 = (bf16[256,2560]{1,0:T(8,128)(2,1)}, bf16[256,2560]{1,0:T(8,128)(2,1)S(1)}, u32[]{:S(2)}, u32[]{:S(2)}) collective-permute-start(bf16[256,2560]{1,0:T(8,128)(2,1)} %get-tuple-element.17), channel_id=1, source_target_pairs={{0,16},{16,0},{1,17},{17,1},{2,18},{18,2},{3,19},{19,3},{4,20},{20... | collective-permute-start | bytes 3932168 | tf_op jit(solution)/shard_map/ppermute | solution.py:25
  38.9 281.2 %reduce-scatter.3.cloned.1.call-start = ((), (), s32[]{:S(2)}) async-start(), calls=%async_computation.5 | async-start | bytes 5160960 | tf_op jit(solution)/shard_map/reduce_scatter | solution.py:257
  39.0 16.4 %collective-permute-start.3 = (bf16[320,448]{1,0:T(8,128)(2,1)}, bf16[320,448]{1,0:T(8,128)(2,1)S(1)}, u32[]{:S(2)}, u32[]{:S(2)}) collective-permute-start(bf16[320,448]{1,0:T(8,128)(2,1)} %param.11), channel_id=1, source_target_pairs={{0,96},{32,0},{64,32},{96,64},{1,97},{33,1},{65,33},{97,65},{2,98}... | collective-permute-start | bytes 860168 | tf_op jit(solution)/shard_map/ppermute | solution.py:21
  46.6 50.5 %collective-permute-start.28 = (bf16[256,2560]{1,0:T(8,128)(2,1)}, bf16[256,2560]{1,0:T(8,128)(2,1)}, u32[]{:S(2)}, u32[]{:S(2)}) collective-permute-start(bf16[256,2560]{1,0:T(8,128)(2,1)} %get-tuple-element.25), channel_id=1, source_target_pairs={{0,16},{16,0},{1,17},{17,1},{2,18},{18,2},{3,19},{19,3},{4,20},{20... | collective-permute-start | bytes 3932168 | tf_op jit(solution)/shard_map/ppermute | solution.py:25
  50.4 17.3 %collective-permute-start.4 = (bf16[320,448]{1,0:T(8,128)(2,1)}, bf16[320,448]{1,0:T(8,128)(2,1)S(1)}, u32[]{:S(2)}, u32[]{:S(2)}) collective-permute-start(bf16[320,448]{1,0:T(8,128)(2,1)} %collective-permute-done), channel_id=1, source_target_pairs={{0,32},{32,64},{64,96},{96,0},{1,33},{33,65},{65,97},{97,1},{2,34}... | collective-permute-start | bytes 860168 | tf_op jit(solution)/shard_map/ppermute | solution.py:21
  50.5 31.7 %collective-permute-start.5 = (bf16[320,448]{1,0:T(8,128)(2,1)S(1)}, bf16[320,448]{1,0:T(8,128)(2,1)S(1)}, u32[]{:S(2)}, u32[]{:S(2)}) collective-permute-start(bf16[320,448]{1,0:T(8,128)(2,1)S(1)} %collective-permute-done.1), channel_id=1, source_target_pairs={{0,32},{32,64},{64,96},{96,0},{1,33},{33,65},{65,97},{97,1},{2,34}... | collective-permute-start | bytes 860168 | tf_op jit(solution)/shard_map/ppermute | solution.py:21
  51.8 30.5 %collective-permute-start.6 = (bf16[320,448]{1,0:T(8,128)(2,1)}, bf16[320,448]{1,0:T(8,128)(2,1)S(1)}, u32[]{:S(2)}, u32[]{:S(2)}) collective-permute-start(bf16[320,448]{1,0:T(8,128)(2,1)} %collective-permute-done.2), channel_id=1, source_target_pairs={{0,96},{32,0},{64,32},{96,64},{1,97},{33,1},{65,33},{97,65},{2,98}... | collective-permute-start | bytes 860168 | tf_op jit(solution)/shard_map/ppermute | solution.py:21
  105.3 39.2 %collective-permute-start.11 = (bf16[320,896]{1,0:T(8,128)(2,1)S(1)}, bf16[320,896]{1,0:T(8,128)(2,1)S(1)}, u32[]{:S(2)}, u32[]{:S(2)}) collective-permute-start(bf16[320,896]{1,0:T(8,128)(2,1)S(1)} %reshape.43), channel_id=1, source_target_pairs={{0,32},{32,64},{64,96},{96,0},{1,33},{33,65},{65,97},{97,1},{2,34}... | collective-permute-start | bytes 1720328 | tf_op jit(solution)/shard_map/ppermute | solution.py:21
  144.5 23.0 %collective-permute-start.17 = (bf16[320,896]{1,0:T(8,128)(2,1)S(1)}, bf16[320,896]{1,0:T(8,128)(2,1)S(1)}, u32[]{:S(2)}, u32[]{:S(2)}) collective-permute-start(bf16[320,896]{1,0:T(8,128)(2,1)S(1)} %collective-permute-done.11), channel_id=1, source_target_pairs={{0,32},{32,64},{64,96},{96,0},{1,33},{33,65},{65,97},{97,1},{2,34}... | collective-permute-start | bytes 1720328 | tf_op jit(solution)/shard_map/ppermute | solution.py:21
  144.5 26.9 %collective-permute-start.19 = (bf16[320,896]{1,0:T(8,128)(2,1)S(1)}, bf16[320,896]{1,0:T(8,128)(2,1)S(1)}, u32[]{:S(2)}, u32[]{:S(2)}) collective-permute-start(bf16[320,896]{1,0:T(8,128)(2,1)S(1)} %reshape.43), channel_id=1, source_target_pairs={{0,96},{32,0},{64,32},{96,64},{1,97},{33,1},{65,33},{97,65},{2,98}... | collective-permute-start | bytes 1720328 | tf_op jit(solution)/shard_map/ppermute | solution.py:21
  147.2 24.2 %collective-permute-start.20 = (bf16[320,896]{1,0:T(8,128)(2,1)S(1)}, bf16[320,896]{1,0:T(8,128)(2,1)S(1)}, u32[]{:S(2)}, u32[]{:S(2)}) collective-permute-start(bf16[320,896]{1,0:T(8,128)(2,1)S(1)} %collective-permute-done.11), channel_id=1, source_target_pairs={{0,128},{128,0},{1,129},{129,1},{2,130},{130,2},{3,131},{131,3},{4... | collective-permute-start | bytes 1720328 | tf_op jit(solution)/shard_map/ppermute | solution.py:25
  167.5 22.5 %collective-permute-start.18 = (bf16[320,896]{1,0:T(8,128)(2,1)S(1)}, bf16[320,896]{1,0:T(8,128)(2,1)S(1)}, u32[]{:S(2)}, u32[]{:S(2)}) collective-permute-start(bf16[320,896]{1,0:T(8,128)(2,1)S(1)} %collective-permute-done.17), channel_id=1, source_target_pairs={{0,128},{128,0},{1,129},{129,1},{2,130},{130,2},{3,131},{131,3},{4... | collective-permute-start | bytes 1720328 | tf_op jit(solution)/shard_map/ppermute | solution.py:25
  171.4 30.9 %collective-permute-start.10 = (bf16[320,896]{1,0:T(8,128)(2,1)S(1)}, bf16[320,896]{1,0:T(8,128)(2,1)S(1)}, u32[]{:S(2)}, u32[]{:S(2)}) collective-permute-start(bf16[320,896]{1,0:T(8,128)(2,1)S(1)} %reshape.43), channel_id=1, source_target_pairs={{0,128},{128,0},{1,129},{129,1},{2,130},{130,2},{3,131},{131,3},{4... | collective-permute-start | bytes 1720328 | tf_op jit(solution)/shard_map/ppermute | solution.py:25
  195.2 17.7 %collective-permute-start.21 = (bf16[128,1280]{1,0:T(8,128)(2,1)}, bf16[128,1280]{1,0:T(8,128)(2,1)S(1)}, u32[]{:S(2)}, u32[]{:S(2)}) collective-permute-start(bf16[128,1280]{1,0:T(8,128)(2,1)} %bitcast.50), channel_id=1, source_target_pairs={{0,1},{1,2},{2,3},{3,0},{4,5},{5,6},{6,7},{7,4},{8,9},{9,10},{10,1... | collective-permute-start | bytes 983048 | tf_op jit(solution)/shard_map/ppermute | solution.py:21
  195.2 17.7 %collective-permute-start.22 = (bf16[128,1280]{1,0:T(8,128)(2,1)}, bf16[128,1280]{1,0:T(8,128)(2,1)S(1)}, u32[]{:S(2)}, u32[]{:S(2)}) collective-permute-start(bf16[128,1280]{1,0:T(8,128)(2,1)} %bitcast.49), channel_id=1, source_target_pairs={{0,2},{1,3},{2,0},{3,1},{4,6},{5,7},{6,4},{7,5},{8,10},{9,11},{10,... | collective-permute-start | bytes 983048 | tf_op jit(solution)/shard_map/ppermute | solution.py:21
  195.2 17.7 %collective-permute-start.23 = (bf16[128,1280]{1,0:T(8,128)(2,1)}, bf16[128,1280]{1,0:T(8,128)(2,1)S(1)}, u32[]{:S(2)}, u32[]{:S(2)}) collective-permute-start(bf16[128,1280]{1,0:T(8,128)(2,1)} %bitcast.48), channel_id=1, source_target_pairs={{0,3},{1,0},{2,1},{3,2},{4,7},{5,4},{6,5},{7,6},{8,11},{9,8},{10,9... | collective-permute-start | bytes 983048 | tf_op jit(solution)/shard_map/ppermute | solution.py:21
  202.3 17.2 %collective-permute-start.12 = (bf16[320,896]{1,0:T(8,128)(2,1)S(1)}, bf16[320,896]{1,0:T(8,128)(2,1)S(1)}, u32[]{:S(2)}, u32[]{:S(2)}) collective-permute-start(bf16[320,896]{1,0:T(8,128)(2,1)S(1)} %collective-permute-done.10), channel_id=1, source_target_pairs={{0,96},{32,0},{64,32},{96,64},{1,97},{33,1},{65,33},{97,65},{2,98}... | collective-permute-start | bytes 1720328 | tf_op jit(solution)/shard_map/ppermute | solution.py:21
  228.6 19.2 %all-to-all-start = ((bf16[4,128,1280]{2,1,0:T(8,128)(2,1)}), bf16[4,128,1280]{2,1,0:T(8,128)(2,1)S(1)}, u32[]{:S(2)}, u32[]{:S(2)}) async-start(bf16[4,128,1280]{2,1,0:T(8,128)(2,1)} %bitcast.17), calls=%async_computation | async-start | bytes 2621440 | tf_op jit(solution)/shard_map/all_to_all | solution.py:230
  248.8 27.4 %all-to-all-start.1 = ((bf16[4,32,1280]{2,1,0:T(8,128)(2,1)}), bf16[4,32,1280]{2,1,0:T(8,128)(2,1)S(1)}, u32[]{:S(2)}, u32[]{:S(2)}) async-start(bf16[4,32,1280]{2,1,0:T(8,128)(2,1)} %bitcast.18), calls=%async_computation.1 | async-start | bytes 655360 | tf_op jit(solution)/shard_map/all_to_all | solution.py:239
  275.9 23.8 %collective-permute-start.25 = (bf16[64,2560]{1,0:T(8,128)(2,1)S(1)}, bf16[64,2560]{1,0:T(8,128)(2,1)S(1)}, u32[]{:S(2)}, u32[]{:S(2)}) collective-permute-start(bf16[64,2560]{1,0:T(8,128)(2,1)S(1)} %all_gather.7.refs_4_), channel_id=1, source_target_pairs={{0,1},{1,2},{2,3},{3,0},{4,5},{5,6},{6,7},{7,4},{8,9},{9,10},{10,1... | collective-permute-start | bytes 983048 | tf_op jit(solution)/shard_map/ppermute | solution.py:21
  280.4 21.2 %collective-permute-start.26 = (bf16[64,2560]{1,0:T(8,128)(2,1)S(1)}, bf16[64,2560]{1,0:T(8,128)(2,1)S(1)}, u32[]{:S(2)}, u32[]{:S(2)}) collective-permute-start(bf16[64,2560]{1,0:T(8,128)(2,1)S(1)} %all_gather.7.refs_4_), channel_id=1, source_target_pairs={{0,2},{1,3},{2,0},{3,1},{4,6},{5,7},{6,4},{7,5},{8,10},{9,11},{10,... | collective-permute-start | bytes 983048 | tf_op jit(solution)/shard_map/ppermute | solution.py:21
  282.2 19.4 %collective-permute-start.27 = (bf16[64,2560]{1,0:T(8,128)(2,1)S(1)}, bf16[64,2560]{1,0:T(8,128)(2,1)S(1)}, u32[]{:S(2)}, u32[]{:S(2)}) collective-permute-start(bf16[64,2560]{1,0:T(8,128)(2,1)S(1)} %all_gather.7.refs_4_), channel_id=1, source_target_pairs={{0,3},{1,0},{2,1},{3,2},{4,7},{5,4},{6,5},{7,6},{8,11},{9,8},{10,9... | collective-permute-start | bytes 983048 | tf_op jit(solution)/shard_map/ppermute | solution.py:21
  299.7 14.3 %collective-permute-start.16 = (bf16[64,2560]{1,0:T(8,128)(2,1)S(1)}, bf16[64,2560]{1,0:T(8,128)(2,1)S(1)}, u32[]{:S(2)}, u32[]{:S(2)}) collective-permute-start(bf16[64,2560]{1,0:T(8,128)(2,1)S(1)} %all_gather.6.refs_0_), channel_id=1, source_target_pairs={{0,3},{1,0},{2,1},{3,2},{4,7},{5,4},{6,5},{7,6},{8,11},{9,8},{10,9... | collective-permute-start | bytes 983048 | tf_op jit(solution)/shard_map/ppermute | solution.py:21
  (33 other events, 399.1 us)
Sparse Core Ops, SparseCore 0:
  39.0 54.8 reduce-scatter.4
  103.9 81.8 reduce-scatter.2

commit v2 on v1

--- a/solution.py
+++ b/solution.py
@@ -192,7 +192,7 @@
     gate_near[3] = shift(gate_near[0], X, -1)
     gate_near[2] = shift(gate_near[1], X, 1)
     gate_far[3] = swap(gate_near[1], Z)
-    gate_far[2] = swap(gate_near[2], Z)
+    gate_far[2] = shift(gate_far[1], X, -1)
 
     out_mine, out_theirs = to_columns(grad_out, pos, slab)
     out_theirs = swap(out_theirs, C)
@@ -206,11 +206,14 @@
     act_all = jnp.concatenate([act_mine, act_theirs])
 
     down = jnp.zeros((2 * nx, slab, width), BF)
-    for h in (0, 1, 3, 2):
+    for h in (0, 1, 3):
         x = (xi - h) & (nx - 1)
         down = lax.dynamic_update_slice(down, near[h][None], (zi * nx + x, 0, 0))
         x = (xi + h) & (nx - 1)
         down = lax.dynamic_update_slice(down, far[h][None], ((1 - zi) * nx + x, 0, 0))
+    x = (xi + 2) & (nx - 1)
+    down = lax.dynamic_update_slice(down, near[2][None], (zi * nx + x, 0, 0))
+    down = lax.dynamic_update_slice(down, far[2][None], ((1 - zi) * nx + x, 0, 0))
     down = down.reshape(2 * nx * slab, width)
     part_h = lax.dot_general(down, out_all, (((0,), (1,)), ((), ())), preferred_element_type=F32)
     got_h = swap(part_h, C)

time: 334 us -> 348 us (1.042)
  waiting for transfers between devices: 167 us -> 177 us
  starting transfers between devices: 59.1 us -> 63.4 us
    ppermute x19 -> x20, waiting for transfers between devices: 112 us -> 128 us  [shift(): return lax.ppermute(v, axis, [(i, (i + step) % n) for i in range(n)])]
    ppermute x10 -> x9, waiting for transfers between devices: 35.1 us -> 27.1 us  [swap(): return lax.ppermute(v, axis, [(0, 1), (1, 0)])]
    all_to_all x2, starting transfers between devices: 9.34 us -> 13.8 us  [layer(): part = lax.all_to_all(part, ZH, 0, 0, tiled=True)]
    ppermute x19 -> x20, starting transfers between devices: 20 us -> 24.3 us  [shift(): return lax.ppermute(v, axis, [(i, (i + step) % n) for i in range(n)])]
    ppermute x10 -> x9, starting transfers between devices: 24.2 us -> 20.5 us  [swap(): return lax.ppermute(v, axis, [(0, 1), (1, 0)])]
  transfers between devices with their start and end apart: 34 -> 34, of which waited for: 16 -> 18; matrix products, arithmetic and copies ran while one was open for 7% -> 7% of each run, Pallas kernels for 6% -> 6%
where the time goes in v2:
time: 348 us; the launch traced here: 344 us
  waiting for transfers between devices  177 us (51%)
  starting transfers between devices  63.4 us (18%)
  blocking collectives  26.8 us (8%)
  Pallas kernels  25 us (7%)
  matrix products  15.6 us (4%)
  local copies, waits for them, and re-layouts  15.2 us (4%)
  between operations  14.4 us (4%)
  other arithmetic  6.56 us (2%)
    ppermute x20, waiting for transfers between devices, shift(): return lax.ppermute(v, axis, [(i, (i + step) % n) for i in range(n)])  128 us
    ppermute x9, waiting for transfers between devices, swap(): return lax.ppermute(v, axis, [(0, 1), (1, 0)])  27.1 us
    all_gather x2, blocking collectives, layer(): piece = lax.all_gather(piece, ZH, axis=0, tiled=True)  26.8 us
    ppermute x20, starting transfers between devices, shift(): return lax.ppermute(v, axis, [(i, (i + step) % n) for i in range(n)])  24.3 us
    ppermute x9, starting transfers between devices, swap(): return lax.ppermute(v, axis, [(0, 1), (1, 0)])  20.5 us
    all_to_all x1, waiting for transfers between devices, layer(): part = lax.all_to_all(part, Y, 0, 0, tiled=True)  15.1 us
    all_to_all x2, starting transfers between devices, layer(): part = lax.all_to_all(part, ZH, 0, 0, tiled=True)  13.8 us
    pallas_call x2, Pallas kernels, to_columns(): pl.pallas_call(functools.partial(to_columns_kernel, slab=slab), grid_spec...  9.92 us
  transfers between devices with their start and end apart: 34, of which 18 were waited for; matrix products, arithmetic and copies ran while one was open for 7% of the time, Pallas kernels for 6%

profile of v2, /device:TPU:1, one launch (start us, length us, event | category | flops | bytes accessed | tf_op | source)
XLA Modules:
  0.0 344.4 jit_solution(13898878366822632602)
XLA Ops:
  7.8 5.0 %to_columns.2 = (bf16[256,2560]{1,0:T(8,128)(2,1)}, bf16[256,2560]{1,0:T(8,128)(2,1)}) custom-call(s32[4]{0:T(128)} %pad_add_fusion.pos_ref, bf16[256,5120]{1,0:T(8,128)(2,1)} %x_ref.2), custom_call_target="tpu_custom_call" | custom-call | tf_op jit(solution)/shard_map/to_columns/pallas_call | solution.py:43
  16.4 9.1 %collective-permute-done = bf16[320,448]{1,0:T(8,128)(2,1)} collective-permute-done((bf16[320,448]{1,0:T(8,128)(2,1)}, bf16[320,448]{1,0:T(8,128)(2,1)}, u32[]{:S(2)}, u32[]{:S(2)}) %collective-permute-start) | collective-permute-done | bytes 286752 | tf_op jit(solution)/shard_map/ppermute | solution.py:25
  30.3 3.8 %collective-permute-done.2 = bf16[320,448]{1,0:T(8,128)(2,1)} collective-permute-done((bf16[320,448]{1,0:T(8,128)(2,1)}, bf16[320,448]{1,0:T(8,128)(2,1)}, u32[]{:S(2)}, u32[]{:S(2)}) %collective-permute-start.2) | collective-permute-done | bytes 286752 | tf_op jit(solution)/shard_map/ppermute | solution.py:21
  41.7 5.0 %to_columns.3 = (bf16[256,2560]{1,0:T(8,128)(2,1)}, bf16[256,2560]{1,0:T(8,128)(2,1)}) custom-call(s32[4]{0:T(128)} %pad_add_fusion.pos_ref, bf16[256,5120]{1,0:T(8,128)(2,1)} %x_ref.3), custom_call_target="tpu_custom_call" | custom-call | tf_op jit(solution)/shard_map/to_columns/pallas_call | solution.py:43
  55.5 12.3 %collective-permute-done.4 = bf16[320,448]{1,0:T(8,128)(2,1)S(1)} collective-permute-done((bf16[320,448]{1,0:T(8,128)(2,1)}, bf16[320,448]{1,0:T(8,128)(2,1)S(1)}, u32[]{:S(2)}, u32[]{:S(2)}) %collective-permute-start.4) | collective-permute-done | bytes 286752 | tf_op jit(solution)/shard_map/ppermute | solution.py:21
  67.8 14.5 %collective-permute-done.5 = bf16[320,448]{1,0:T(8,128)(2,1)S(1)} collective-permute-done((bf16[320,448]{1,0:T(8,128)(2,1)S(1)}, bf16[320,448]{1,0:T(8,128)(2,1)S(1)}, u32[]{:S(2)}, u32[]{:S(2)}) %collective-permute-start.5) | collective-permute-done | bytes 286752 | tf_op jit(solution)/shard_map/ppermute | solution.py:21
  84.1 6.8 %collective-permute-start.8 = (f32[448,512]{1,0:T(8,128)S(1)}, f32[448,512]{1,0:T(8,128)S(1)}, u32[]{:S(2)}, u32[]{:S(2)}) collective-permute-start(f32[448,512]{1,0:T(8,128)S(1)} %fusion.25.part_ref), channel_id=1, source_target_pairs={{0,16},{16,0},{1,17},{17,1},{2,18},{18,2},{3,19},{19,3},{4,20},{20... | collective-permute-start | bytes 2752520 | tf_op jit(solution)/shard_map/ppermute | solution.py:25
  97.1 6.6 %convolution_convert_fusion = bf16[2560,896]{1,0:T(8,128)(2,1)} fusion(bf16[896,512]{1,0:T(8,128)(2,1)} %grad_hidden.1, bf16[256,2560]{1,0:T(8,128)(2,1)} %collective-permute-done.28, bf16[256,2560]{1,0:T(8,128)(2,1)S(1)} %copy-done.21), kind=kOutput, calls=%fused_computation | convolution fusion | flops 2356346880 | bytes 8126464 | tf_op jit(solution)/shard_map/dot_general | solution.py:257
  107.5 15.0 %collective-permute-done.10 = bf16[320,896]{1,0:T(8,128)(2,1)S(1)} collective-permute-done((bf16[320,896]{1,0:T(8,128)(2,1)S(1)}, bf16[320,896]{1,0:T(8,128)(2,1)S(1)}, u32[]{:S(2)}, u32[]{:S(2)}) %collective-permute-start.10) | collective-permute-done | bytes 573472 | tf_op jit(solution)/shard_map/ppermute | solution.py:25
  122.5 13.1 %collective-permute-done.11 = bf16[320,896]{1,0:T(8,128)(2,1)S(1)} collective-permute-done((bf16[320,896]{1,0:T(8,128)(2,1)S(1)}, bf16[320,896]{1,0:T(8,128)(2,1)S(1)}, u32[]{:S(2)}, u32[]{:S(2)}) %collective-permute-start.11) | collective-permute-done | bytes 573472 | tf_op jit(solution)/shard_map/ppermute | solution.py:21
  136.0 23.8 %collective-permute-done.12 = bf16[320,896]{1,0:T(8,128)(2,1)S(1)} collective-permute-done((bf16[320,896]{1,0:T(8,128)(2,1)S(1)}, bf16[320,896]{1,0:T(8,128)(2,1)S(1)}, u32[]{:S(2)}, u32[]{:S(2)}) %collective-permute-start.12) | collective-permute-done | bytes 573472 | tf_op jit(solution)/shard_map/ppermute | solution.py:21
  159.8 3.9 %collective-permute-start.18 = (bf16[320,896]{1,0:T(8,128)(2,1)S(1)}, bf16[320,896]{1,0:T(8,128)(2,1)S(1)}, u32[]{:S(2)}, u32[]{:S(2)}) collective-permute-start(bf16[320,896]{1,0:T(8,128)(2,1)S(1)} %collective-permute-done.12), channel_id=1, source_target_pairs={{0,96},{32,0},{64,32},{96,64},{1,97},{33,1},{65,33},{97,65},{2,98}... | collective-permute-start | bytes 1720328 | tf_op jit(solution)/shard_map/ppermute | solution.py:21
  163.7 21.3 %collective-permute-done.19 = bf16[320,896]{1,0:T(8,128)(2,1)S(1)} collective-permute-done((bf16[320,896]{1,0:T(8,128)(2,1)S(1)}, bf16[320,896]{1,0:T(8,128)(2,1)S(1)}, u32[]{:S(2)}, u32[]{:S(2)}) %collective-permute-start.19) | collective-permute-done | bytes 573472 | tf_op jit(solution)/shard_map/ppermute | solution.py:21
  185.0 14.7 %collective-permute-done.18 = bf16[320,896]{1,0:T(8,128)(2,1)S(1)} collective-permute-done((bf16[320,896]{1,0:T(8,128)(2,1)S(1)}, bf16[320,896]{1,0:T(8,128)(2,1)S(1)}, u32[]{:S(2)}, u32[]{:S(2)}) %collective-permute-start.18) | collective-permute-done | bytes 573472 | tf_op jit(solution)/shard_map/ppermute | solution.py:21
  210.8 5.5 %collective-permute-done.21 = bf16[128,1280]{1,0:T(8,128)(2,1)S(1)} collective-permute-done((bf16[128,1280]{1,0:T(8,128)(2,1)}, bf16[128,1280]{1,0:T(8,128)(2,1)S(1)}, u32[]{:S(2)}, u32[]{:S(2)}) %collective-permute-start.21) | collective-permute-done | bytes 327712 | tf_op jit(solution)/shard_map/ppermute | solution.py:21
  216.3 7.9 %collective-permute-done.22 = bf16[128,1280]{1,0:T(8,128)(2,1)S(1)} collective-permute-done((bf16[128,1280]{1,0:T(8,128)(2,1)}, bf16[128,1280]{1,0:T(8,128)(2,1)S(1)}, u32[]{:S(2)}, u32[]{:S(2)}) %collective-permute-start.22) | collective-permute-done | bytes 327712 | tf_op jit(solution)/shard_map/ppermute | solution.py:21
  226.1 6.9 %all-to-all-start.2 = ((bf16[4,32,1280]{2,1,0:T(8,128)(2,1)}), bf16[4,32,1280]{2,1,0:T(8,128)(2,1)S(1)}, u32[]{:S(2)}, u32[]{:S(2)}) async-start(bf16[4,32,1280]{2,1,0:T(8,128)(2,1)} %bitcast.24), calls=%async_computation.2 | async-start | bytes 655360 | tf_op jit(solution)/shard_map/all_to_all | solution.py:242
  235.7 6.8 %all-to-all-done.2 = bf16[4,32,1280]{2,1,0:T(8,128)(2,1)S(1)} async-done(((bf16[4,32,1280]{2,1,0:T(8,128)(2,1)}), bf16[4,32,1280]{2,1,0:T(8,128)(2,1)S(1)}, u32[]{:S(2)}, u32[]{:S(2)}) %all-to-all-start.2) | async-done | bytes 327712 | tf_op jit(solution)/shard_map/all_to_all | solution.py:242
  242.5 4.7 %all-to-all-start = ((bf16[4,128,1280]{2,1,0:T(8,128)(2,1)}), bf16[4,128,1280]{2,1,0:T(8,128)(2,1)S(1)}, u32[]{:S(2)}, u32[]{:S(2)}) async-start(bf16[4,128,1280]{2,1,0:T(8,128)(2,1)} %bitcast.17), calls=%async_computation | async-start | bytes 2621440 | tf_op jit(solution)/shard_map/all_to_all | solution.py:233
  247.2 15.1 %all-to-all-done = bf16[4,128,1280]{2,1,0:T(8,128)(2,1)S(1)} async-done(((bf16[4,128,1280]{2,1,0:T(8,128)(2,1)}), bf16[4,128,1280]{2,1,0:T(8,128)(2,1)S(1)}, u32[]{:S(2)}, u32[]{:S(2)}) %all-to-all-start) | async-done | bytes 1310752 | tf_op jit(solution)/shard_map/all_to_all | solution.py:233
  263.4 6.9 %all-to-all-start.1 = ((bf16[4,32,1280]{2,1,0:T(8,128)(2,1)}), bf16[4,32,1280]{2,1,0:T(8,128)(2,1)S(1)}, u32[]{:S(2)}, u32[]{:S(2)}) async-start(bf16[4,32,1280]{2,1,0:T(8,128)(2,1)} %bitcast.18), calls=%async_computation.1 | async-start | bytes 655360 | tf_op jit(solution)/shard_map/all_to_all | solution.py:242
  275.9 14.3 %all_gather.7.refs_4_ = bf16[64,2560]{1,0:T(8,128)(2,1)S(1)} all-gather(bf16[16,2560]{1,0:T(8,128)(2,1)} %from_slabs.3), channel_id=1, replica_groups=mesh['dp_0'=2,'dp_1'=4,'dp_2'=2,'tensor_0'=4,'tensor_1'=4] {'tensor_0'}, dimensions={0}, use_global_device_ids=true | all-gather | bytes 409600 | tf_op jit(solution)/shard_map/all_gather | solution.py:246
  299.1 12.6 %all_gather.6.refs_0_ = bf16[64,2560]{1,0:T(8,128)(2,1)S(1)} all-gather(bf16[16,2560]{1,0:T(8,128)(2,1)} %from_slabs.2), channel_id=1, replica_groups=mesh['dp_0'=2,'dp_1'=4,'dp_2'=2,'tensor_0'=4,'tensor_1'=4] {'tensor_0'}, dimensions={0}, use_global_device_ids=true | all-gather | bytes 409600 | tf_op jit(solution)/shard_map/all_gather | solution.py:246
  319.2 8.0 %collective-permute-done.15.refs_2_ = bf16[64,2560]{1,0:T(8,128)(2,1)S(1)} collective-permute-done((bf16[64,2560]{1,0:T(8,128)(2,1)S(1)}, bf16[64,2560]{1,0:T(8,128)(2,1)S(1)}, u32[]{:S(2)}, u32[]{:S(2)}) %collective-permute-start.15) | collective-permute-done | bytes 327712 | tf_op jit(solution)/shard_map/ppermute | solution.py:21
  (131 shorter events, 86.5 us)
Async XLA Ops:
  7.2 325.1 %reduce-scatter.5.cloned.1.call-start = ((), (), s32[]{:S(2)}) async-start(), calls=%async_computation.6 | async-start | bytes 2949120 | tf_op jit(solution)/shard_map/reduce_scatter | solution.py:255
  12.8 21.4 %collective-permute-start.7 = (bf16[256,2560]{1,0:T(8,128)(2,1)}, bf16[256,2560]{1,0:T(8,128)(2,1)S(1)}, u32[]{:S(2)}, u32[]{:S(2)}) collective-permute-start(bf16[256,2560]{1,0:T(8,128)(2,1)} %get-tuple-element.17), channel_id=1, source_target_pairs={{0,16},{16,0},{1,17},{17,1},{2,18},{18,2},{3,19},{19,3},{4,20},{20... | collective-permute-start | bytes 3932168 | tf_op jit(solution)/shard_map/ppermute | solution.py:25
  38.9 295.2 %reduce-scatter.3.cloned.1.call-start = ((), (), s32[]{:S(2)}) async-start(), calls=%async_computation.5 | async-start | bytes 5160960 | tf_op jit(solution)/shard_map/reduce_scatter | solution.py:260
  39.0 16.4 %collective-permute-start.3 = (bf16[320,448]{1,0:T(8,128)(2,1)}, bf16[320,448]{1,0:T(8,128)(2,1)S(1)}, u32[]{:S(2)}, u32[]{:S(2)}) collective-permute-start(bf16[320,448]{1,0:T(8,128)(2,1)} %param.11), channel_id=1, source_target_pairs={{0,96},{32,0},{64,32},{96,64},{1,97},{33,1},{65,33},{97,65},{2,98}... | collective-permute-start | bytes 860168 | tf_op jit(solution)/shard_map/ppermute | solution.py:21
  46.6 50.5 %collective-permute-start.28 = (bf16[256,2560]{1,0:T(8,128)(2,1)}, bf16[256,2560]{1,0:T(8,128)(2,1)}, u32[]{:S(2)}, u32[]{:S(2)}) collective-permute-start(bf16[256,2560]{1,0:T(8,128)(2,1)} %get-tuple-element.25), channel_id=1, source_target_pairs={{0,16},{16,0},{1,17},{17,1},{2,18},{18,2},{3,19},{19,3},{4,20},{20... | collective-permute-start | bytes 3932168 | tf_op jit(solution)/shard_map/ppermute | solution.py:25
  50.4 17.3 %collective-permute-start.4 = (bf16[320,448]{1,0:T(8,128)(2,1)}, bf16[320,448]{1,0:T(8,128)(2,1)S(1)}, u32[]{:S(2)}, u32[]{:S(2)}) collective-permute-start(bf16[320,448]{1,0:T(8,128)(2,1)} %collective-permute-done), channel_id=1, source_target_pairs={{0,32},{32,64},{64,96},{96,0},{1,33},{33,65},{65,97},{97,1},{2,34}... | collective-permute-start | bytes 860168 | tf_op jit(solution)/shard_map/ppermute | solution.py:21
  50.5 31.7 %collective-permute-start.5 = (bf16[320,448]{1,0:T(8,128)(2,1)S(1)}, bf16[320,448]{1,0:T(8,128)(2,1)S(1)}, u32[]{:S(2)}, u32[]{:S(2)}) collective-permute-start(bf16[320,448]{1,0:T(8,128)(2,1)S(1)} %collective-permute-done.1), channel_id=1, source_target_pairs={{0,32},{32,64},{64,96},{96,0},{1,33},{33,65},{65,97},{97,1},{2,34}... | collective-permute-start | bytes 860168 | tf_op jit(solution)/shard_map/ppermute | solution.py:21
  51.8 30.5 %collective-permute-start.6 = (bf16[320,448]{1,0:T(8,128)(2,1)}, bf16[320,448]{1,0:T(8,128)(2,1)S(1)}, u32[]{:S(2)}, u32[]{:S(2)}) collective-permute-start(bf16[320,448]{1,0:T(8,128)(2,1)} %collective-permute-done.2), channel_id=1, source_target_pairs={{0,96},{32,0},{64,32},{96,64},{1,97},{33,1},{65,33},{97,65},{2,98}... | collective-permute-start | bytes 860168 | tf_op jit(solution)/shard_map/ppermute | solution.py:21
  105.3 17.2 %collective-permute-start.10 = (bf16[320,896]{1,0:T(8,128)(2,1)S(1)}, bf16[320,896]{1,0:T(8,128)(2,1)S(1)}, u32[]{:S(2)}, u32[]{:S(2)}) collective-permute-start(bf16[320,896]{1,0:T(8,128)(2,1)S(1)} %reshape.43), channel_id=1, source_target_pairs={{0,128},{128,0},{1,129},{129,1},{2,130},{130,2},{3,131},{131,3},{4... | collective-permute-start | bytes 1720328 | tf_op jit(solution)/shard_map/ppermute | solution.py:25
  107.5 28.1 %collective-permute-start.11 = (bf16[320,896]{1,0:T(8,128)(2,1)S(1)}, bf16[320,896]{1,0:T(8,128)(2,1)S(1)}, u32[]{:S(2)}, u32[]{:S(2)}) collective-permute-start(bf16[320,896]{1,0:T(8,128)(2,1)S(1)} %reshape.43), channel_id=1, source_target_pairs={{0,32},{32,64},{64,96},{96,0},{1,33},{33,65},{65,97},{97,1},{2,34}... | collective-permute-start | bytes 1720328 | tf_op jit(solution)/shard_map/ppermute | solution.py:21
  122.5 37.3 %collective-permute-start.12 = (bf16[320,896]{1,0:T(8,128)(2,1)S(1)}, bf16[320,896]{1,0:T(8,128)(2,1)S(1)}, u32[]{:S(2)}, u32[]{:S(2)}) collective-permute-start(bf16[320,896]{1,0:T(8,128)(2,1)S(1)} %collective-permute-done.10), channel_id=1, source_target_pairs={{0,96},{32,0},{64,32},{96,64},{1,97},{33,1},{65,33},{97,65},{2,98}... | collective-permute-start | bytes 1720328 | tf_op jit(solution)/shard_map/ppermute | solution.py:21
  122.5 62.5 %collective-permute-start.19 = (bf16[320,896]{1,0:T(8,128)(2,1)S(1)}, bf16[320,896]{1,0:T(8,128)(2,1)S(1)}, u32[]{:S(2)}, u32[]{:S(2)}) collective-permute-start(bf16[320,896]{1,0:T(8,128)(2,1)S(1)} %reshape.43), channel_id=1, source_target_pairs={{0,96},{32,0},{64,32},{96,64},{1,97},{33,1},{65,33},{97,65},{2,98}... | collective-permute-start | bytes 1720328 | tf_op jit(solution)/shard_map/ppermute | solution.py:21
  135.6 49.4 %collective-permute-start.17 = (bf16[320,896]{1,0:T(8,128)(2,1)S(1)}, bf16[320,896]{1,0:T(8,128)(2,1)S(1)}, u32[]{:S(2)}, u32[]{:S(2)}) collective-permute-start(bf16[320,896]{1,0:T(8,128)(2,1)S(1)} %collective-permute-done.11), channel_id=1, source_target_pairs={{0,32},{32,64},{64,96},{96,0},{1,33},{33,65},{65,97},{97,1},{2,34}... | collective-permute-start | bytes 1720328 | tf_op jit(solution)/shard_map/ppermute | solution.py:21
  135.6 49.4 %collective-permute-start.20 = (bf16[320,896]{1,0:T(8,128)(2,1)S(1)}, bf16[320,896]{1,0:T(8,128)(2,1)S(1)}, u32[]{:S(2)}, u32[]{:S(2)}) collective-permute-start(bf16[320,896]{1,0:T(8,128)(2,1)S(1)} %collective-permute-done.11), channel_id=1, source_target_pairs={{0,128},{128,0},{1,129},{129,1},{2,130},{130,2},{3,131},{131,3},{4... | collective-permute-start | bytes 1720328 | tf_op jit(solution)/shard_map/ppermute | solution.py:25
  159.8 39.9 %collective-permute-start.18 = (bf16[320,896]{1,0:T(8,128)(2,1)S(1)}, bf16[320,896]{1,0:T(8,128)(2,1)S(1)}, u32[]{:S(2)}, u32[]{:S(2)}) collective-permute-start(bf16[320,896]{1,0:T(8,128)(2,1)S(1)} %collective-permute-done.12), channel_id=1, source_target_pairs={{0,96},{32,0},{64,32},{96,64},{1,97},{33,1},{65,33},{97,65},{2,98}... | collective-permute-start | bytes 1720328 | tf_op jit(solution)/shard_map/ppermute | solution.py:21
  207.1 17.1 %collective-permute-start.22 = (bf16[128,1280]{1,0:T(8,128)(2,1)}, bf16[128,1280]{1,0:T(8,128)(2,1)S(1)}, u32[]{:S(2)}, u32[]{:S(2)}) collective-permute-start(bf16[128,1280]{1,0:T(8,128)(2,1)} %bitcast.49), channel_id=1, source_target_pairs={{0,2},{1,3},{2,0},{3,1},{4,6},{5,7},{6,4},{7,5},{8,10},{9,11},{10,... | collective-permute-start | bytes 983048 | tf_op jit(solution)/shard_map/ppermute | solution.py:21
  209.7 14.5 %collective-permute-start.23 = (bf16[128,1280]{1,0:T(8,128)(2,1)}, bf16[128,1280]{1,0:T(8,128)(2,1)S(1)}, u32[]{:S(2)}, u32[]{:S(2)}) collective-permute-start(bf16[128,1280]{1,0:T(8,128)(2,1)} %bitcast.48), channel_id=1, source_target_pairs={{0,3},{1,0},{2,1},{3,2},{4,7},{5,4},{6,5},{7,6},{8,11},{9,8},{10,9... | collective-permute-start | bytes 983048 | tf_op jit(solution)/shard_map/ppermute | solution.py:21
  226.1 16.4 %all-to-all-start.2 = ((bf16[4,32,1280]{2,1,0:T(8,128)(2,1)}), bf16[4,32,1280]{2,1,0:T(8,128)(2,1)S(1)}, u32[]{:S(2)}, u32[]{:S(2)}) async-start(bf16[4,32,1280]{2,1,0:T(8,128)(2,1)} %bitcast.24), calls=%async_computation.2 | async-start | bytes 655360 | tf_op jit(solution)/shard_map/all_to_all | solution.py:242
  242.5 19.9 %all-to-all-start = ((bf16[4,128,1280]{2,1,0:T(8,128)(2,1)}), bf16[4,128,1280]{2,1,0:T(8,128)(2,1)S(1)}, u32[]{:S(2)}, u32[]{:S(2)}) async-start(bf16[4,128,1280]{2,1,0:T(8,128)(2,1)} %bitcast.17), calls=%async_computation | async-start | bytes 2621440 | tf_op jit(solution)/shard_map/all_to_all | solution.py:233
  263.4 27.1 %all-to-all-start.1 = ((bf16[4,32,1280]{2,1,0:T(8,128)(2,1)}), bf16[4,32,1280]{2,1,0:T(8,128)(2,1)S(1)}, u32[]{:S(2)}, u32[]{:S(2)}) async-start(bf16[4,32,1280]{2,1,0:T(8,128)(2,1)} %bitcast.18), calls=%async_computation.1 | async-start | bytes 655360 | tf_op jit(solution)/shard_map/all_to_all | solution.py:242
  290.2 24.4 %collective-permute-start.25 = (bf16[64,2560]{1,0:T(8,128)(2,1)S(1)}, bf16[64,2560]{1,0:T(8,128)(2,1)S(1)}, u32[]{:S(2)}, u32[]{:S(2)}) collective-permute-start(bf16[64,2560]{1,0:T(8,128)(2,1)S(1)} %all_gather.7.refs_4_), channel_id=1, source_target_pairs={{0,1},{1,2},{2,3},{3,0},{4,5},{5,6},{6,7},{7,4},{8,9},{9,10},{10,1... | collective-permute-start | bytes 983048 | tf_op jit(solution)/shard_map/ppermute | solution.py:21
  294.5 22.2 %collective-permute-start.26 = (bf16[64,2560]{1,0:T(8,128)(2,1)S(1)}, bf16[64,2560]{1,0:T(8,128)(2,1)S(1)}, u32[]{:S(2)}, u32[]{:S(2)}) collective-permute-start(bf16[64,2560]{1,0:T(8,128)(2,1)S(1)} %all_gather.7.refs_4_), channel_id=1, source_target_pairs={{0,2},{1,3},{2,0},{3,1},{4,6},{5,7},{6,4},{7,5},{8,10},{9,11},{10,... | collective-permute-start | bytes 983048 | tf_op jit(solution)/shard_map/ppermute | solution.py:21
  296.2 20.4 %collective-permute-start.27 = (bf16[64,2560]{1,0:T(8,128)(2,1)S(1)}, bf16[64,2560]{1,0:T(8,128)(2,1)S(1)}, u32[]{:S(2)}, u32[]{:S(2)}) collective-permute-start(bf16[64,2560]{1,0:T(8,128)(2,1)S(1)} %all_gather.7.refs_4_), channel_id=1, source_target_pairs={{0,3},{1,0},{2,1},{3,2},{4,7},{5,4},{6,5},{7,6},{8,11},{9,8},{10,9... | collective-permute-start | bytes 983048 | tf_op jit(solution)/shard_map/ppermute | solution.py:21
  313.1 14.1 %collective-permute-start.15 = (bf16[64,2560]{1,0:T(8,128)(2,1)S(1)}, bf16[64,2560]{1,0:T(8,128)(2,1)S(1)}, u32[]{:S(2)}, u32[]{:S(2)}) collective-permute-start(bf16[64,2560]{1,0:T(8,128)(2,1)S(1)} %all_gather.6.refs_0_), channel_id=1, source_target_pairs={{0,2},{1,3},{2,0},{3,1},{4,6},{5,7},{6,4},{7,5},{8,10},{9,11},{10,... | collective-permute-start | bytes 983048 | tf_op jit(solution)/shard_map/ppermute | solution.py:21
  (33 other events, 398.9 us)
Sparse Core Ops, SparseCore 0:
  39.0 54.8 reduce-scatter.4
  103.9 94.2 reduce-scatter.2
